TPU v7x, 768 devices: a whole 4x8x12 slice. The times are simulated.
768 devices in a mesh: gx: 16 (over x, y_lo, core), gy: 48 (over y_hi, z).
Axes of the slice: x: 4, y: 8 (y_hi: 4, y_lo: 2; y = y_hi * 2 + y_lo), z: 12, core: 2. Of those that a mesh axis runs over, the one named last changes fastest.
Arguments:
- fields: float32 [5, 32, 128, 6144], P(None, None, 'gx', 'gy'), may hold values from -20 to 20, as said below
- coriolis: float32 [128], P('gx'), may hold values from 0.5 to 1.5
- slope_east: float32 [128, 6144], P('gx', 'gy'), may hold values from -3 to 3
- slope_north: float32 [128, 6144], P('gx', 'gy'), may hold values from -3 to 3
Outputs:
- updated: float32 [4, 32, 128, 6144], P(None, None, 'gx', 'gy')
Inputs may be any that keep to these rules, and one draw needn't show every extreme that they name: `fields`: components in order: velocity along x, velocity along y, vertical velocity, potential temperature, pressure perturbation.
All inputs are finite; a program needn't handle non-finite values.
Results may differ from a plain program's by a relative error of at most 0.0003.
Values sent between devices are 32-bit elements; how exact they have to be, the bound alone decides.
A program may use at most 32 MiB of HBM per device.

v0:
```python
import jax
import jax.numpy as jnp
from jax import lax
from jax.sharding import Mesh
from jax.sharding import PartitionSpec as P

GX_GY = ("gx_0", "gx_1", "gx_2", "gy_0", "gy_1")
GX = ("gx_0", "gx_1", "gx_2")
GY = ("gy_0", "gy_1")


WENO_EPS = 1e-06
SECTION_DT = 0.3
SMAG_COEF = 0.06
BACKGROUND = 0.05
BUOYANCY = 0.5


def one_axis_at_a_time(x, axes):
    for axis in axes:
        x = lax.psum(x, axis)
    return x


def padded(block, sides, width):
    for axis, dim in sides:
        count = lax.axis_size(axis)
        forward = [(i, i + 1) for i in range(count - 1)]
        backward = [(target, source) for source, target in forward]
        low = lax.ppermute(
            lax.slice_in_dim(block, block.shape[dim] - width, None, axis=dim), axis, forward
        )
        high = lax.ppermute(lax.slice_in_dim(block, 0, width, axis=dim), axis, backward)
        block = jnp.concatenate([low, block, high], axis=dim)
    return block


def window(array, start, length, axis):
    return lax.slice_in_dim(array, start, start + length, axis=axis)


def weno_face(outer_low, inner_low, middle, inner_high, outer_high):
    smooth_zero = (
        13.0 / 12.0 * (outer_low - 2.0 * inner_low + middle) ** 2
        + 0.25 * (outer_low - 4.0 * inner_low + 3.0 * middle) ** 2
    )
    smooth_one = (
        13.0 / 12.0 * (inner_low - 2.0 * middle + inner_high) ** 2
        + 0.25 * (inner_low - inner_high) ** 2
    )
    smooth_two = (
        13.0 / 12.0 * (middle - 2.0 * inner_high + outer_high) ** 2
        + 0.25 * (3.0 * middle - 4.0 * inner_high + outer_high) ** 2
    )
    guess_zero = (2.0 * outer_low - 7.0 * inner_low + 11.0 * middle) / 6.0
    guess_one = (-inner_low + 5.0 * middle + 2.0 * inner_high) / 6.0
    guess_two = (2.0 * middle + 5.0 * inner_high - outer_high) / 6.0
    weight_zero = 0.1 / (WENO_EPS + smooth_zero) ** 2
    weight_one = 0.6 / (WENO_EPS + smooth_one) ** 2
    weight_two = 0.3 / (WENO_EPS + smooth_two) ** 2
    total = weight_zero + weight_one + weight_two
    return (weight_zero * guess_zero + weight_one * guess_one + weight_two * guess_two) / total


def faces_along(values, speed, axis, count):
    parts = [window(values, offset, count + 1, axis) for offset in range(6)]
    low_side = weno_face(parts[0], parts[1], parts[2], parts[3], parts[4])
    high_side = weno_face(parts[5], parts[4], parts[3], parts[2], parts[1])
    face_speed = (window(speed, 2, count + 1, axis) + window(speed, 3, count + 1, axis)) * 0.5
    return jnp.maximum(face_speed, 0.0) * low_side + jnp.minimum(face_speed, 0.0) * high_side


def divergence(flux, axis, count):
    return window(flux, 1, count, axis) - window(flux, 0, count, axis)


def section_update(extended, pressure, coriolis, slope_east, slope_north, theta_mean):
    depth = extended.shape[1]
    rows = extended.shape[2] - 6
    cols = extended.shape[3] - 6
    centre = extended[:, :, 3:-3, 3:-3]
    along_x = extended[:, :, 3:-3, :]
    flux_x = faces_along(along_x, along_x[0:1], 3, cols)
    along_y = extended[:, :, :, 3:-3]
    flux_y = faces_along(along_y, along_y[1:2], 2, rows)
    padded_z = jnp.pad(centre, ((0, 0), (3, 3), (0, 0), (0, 0)), mode="edge")
    flux_z = faces_along(padded_z, padded_z[2:3], 1, depth)
    face_index = lax.broadcasted_iota(jnp.int32, (1, depth + 1, 1, 1), 1)
    inside = jnp.logical_and(face_index > 0, face_index < depth).astype(flux_z.dtype)
    flux_z = flux_z * inside
    advection = -(
        divergence(flux_x, 3, cols) + divergence(flux_y, 2, rows) + divergence(flux_z, 1, depth)
    )
    speed_x = extended[0]
    speed_y = extended[1]
    strain_xx = (speed_x[:, 2:-2, 3:-1] - speed_x[:, 2:-2, 1:-3]) * 0.5
    strain_yy = (speed_y[:, 3:-1, 2:-2] - speed_y[:, 1:-3, 2:-2]) * 0.5
    shear = (speed_x[:, 3:-1, 2:-2] - speed_x[:, 1:-3, 2:-2]) * 0.5 + (
        speed_y[:, 2:-2, 3:-1] - speed_y[:, 2:-2, 1:-3]
    ) * 0.5
    eddy = SMAG_COEF * jnp.sqrt(
        2.0 * (strain_xx * strain_xx + strain_yy * strain_yy) + shear * shear + BACKGROUND
    )
    border = extended[:, :, 2:-2, 2:-2]
    eddy_x = (eddy[:, 1:-1, 1:] + eddy[:, 1:-1, :-1]) * 0.5
    diffuse_x = eddy_x * (border[:, :, 1:-1, 1:] - border[:, :, 1:-1, :-1])
    eddy_y = (eddy[:, 1:, 1:-1] + eddy[:, :-1, 1:-1]) * 0.5
    diffuse_y = eddy_y * (border[:, :, 1:, 1:-1] - border[:, :, :-1, 1:-1])
    mixing = (
        diffuse_x[:, :, :, 1:]
        - diffuse_x[:, :, :, :-1]
        + diffuse_y[:, :, 1:, :]
        - diffuse_y[:, :, :-1, :]
    )
    press_x = (pressure[:, 1:-1, 2:] - pressure[:, 1:-1, :-2]) * 0.5
    press_y = (pressure[:, 2:, 1:-1] - pressure[:, :-2, 1:-1]) * 0.5
    column = jnp.pad(pressure[:, 1:-1, 1:-1], ((1, 1), (0, 0), (0, 0)), mode="edge")
    press_z = (column[2:] - column[:-2]) * 0.5
    level_index = lax.broadcasted_iota(jnp.int32, (depth, 1, 1), 0).astype(centre.dtype)
    level_factor = 1.0 - (level_index + 0.5) / depth
    turning = coriolis[None, :, None]
    force_u = -(press_x - slope_east[None] * level_factor * press_z) + turning * centre[1]
    force_v = -(press_y - slope_north[None] * level_factor * press_z) - turning * centre[0]
    force_w = -press_z + BUOYANCY * (centre[3] - theta_mean[:, None, None])
    forcing = jnp.stack([force_u, force_v, force_w, jnp.zeros_like(force_w)])
    return centre + SECTION_DT * (advection + mixing + forcing)


def body(fields, coriolis, slope_east, slope_north):
    level_total = one_axis_at_a_time(jnp.sum(fields[3], axis=(1, 2)), GX_GY)
    cells = fields.shape[2] * fields.shape[3] * lax.axis_size(GX) * lax.axis_size(GY)
    theta_mean = level_total / cells
    widened = padded(fields, ((GY, 3),), 3)
    extended = padded(widened, ((GX, 2),), 3)
    pressure = extended[4, :, 2:-2, 2:-2]
    advected = extended[:4]
    return section_update(advected, pressure, coriolis, slope_east, slope_north, theta_mean)


def solution(mesh):
    finer = Mesh(mesh.devices.reshape(4, 2, 2, 4, 12), ("gx_0", "gx_1", "gx_2", "gy_0", "gy_1"))
    in_specs = (P(None, None, GX, GY), P(GX), P(GX, GY), P(GX, GY))
    out_specs = P(None, None, GX, GY)
    return jax.shard_map(body, mesh=finer, in_specs=in_specs, out_specs=out_specs, check_vma=False)
```

profile of v0, /device:TPU:1, one launch (start us, length us, event | category | flops | bytes accessed | tf_op | source)
XLA Modules:
  0.0 110.2 jit_solution(17032157762023083661)
XLA Ops:
  0.0 0.0 copy-start
  0.0 1.6 %fusion.140 = (f32[5,32,8,3]{3,2,1,0:T(8,128)S(1)}, f32[5,32,8,3]{3,2,1,0:T(8,128)S(1)}) fusion(f32[5,32,8,128]{3,2,1,0:T(8,128)} %param.4), kind=kLoop, calls=%fused_computation.217 | loop fusion | bytes 61440 | tf_op jit(solution)/shard_map/slice | solution.py:31
  1.6 0.3 copy.31
  1.9 4.8 %collective-permute-start = (f32[5,32,8,3]{1,2,3,0:T(8,128)S(1)}, f32[5,32,8,3]{1,2,3,0:T(8,128)S(1)}, u32[]{:S(2)}, u32[]{:S(2)}) collective-permute-start(f32[5,32,8,3]{1,2,3,0:T(8,128)S(1)} %copy.31), channel_id=1, source_target_pairs={{0,1},{1,2},{2,3},{3,4},{4,5},{5,6},{6,7},{7,8},{8,9},{9,10},{10,1... | collective-permute-start | bytes 46088 | tf_op jit(solution)/shard_map/ppermute | solution.py:30
  6.7 0.3 copy.32
  7.1 1.3 %collective-permute-start.1 = (f32[5,32,8,3]{1,2,3,0:T(8,128)S(1)}, f32[5,32,8,3]{1,2,3,0:T(8,128)S(1)}, u32[]{:S(2)}, u32[]{:S(2)}) collective-permute-start(f32[5,32,8,3]{1,2,3,0:T(8,128)S(1)} %copy.32), channel_id=1, source_target_pairs={{1,0},{2,1},{3,2},{4,3},{5,4},{6,5},{7,6},{8,7},{9,8},{10,9},{11,1... | collective-permute-start | bytes 46088 | tf_op jit(solution)/shard_map/ppermute | solution.py:33
  8.4 0.0 copy-done
  8.4 0.3 slice_reduce_fusion
  8.7 8.5 %psum.35 = f32[32]{0:T(128)S(1)} all-reduce(f32[32]{0:T(128)S(1)} %slice_reduce_fusion), channel_id=1, replica_groups=mesh['gx_0'=4,'gx_1'=2,'gx_2'=2,'gy_0'=4,'gy_1'=12] {'gx_0'}, use_global_device_ids=true, to_apply=%region_1.0 | all-reduce | flops 32 | bytes 256 | tf_op jit(solution)/shard_map/psum | solution.py:21
  17.2 4.1 %psum.36 = f32[32]{0:T(128)S(1)} all-reduce(f32[32]{0:T(128)S(1)} %psum.35), channel_id=1, replica_groups=mesh['gx_0'=4,'gx_1'=2,'gx_2'=2,'gy_0'=4,'gy_1'=12] {'gx_1'}, use_global_device_ids=true, to_apply=%region_2.0 | all-reduce | flops 32 | bytes 256 | tf_op jit(solution)/shard_map/psum | solution.py:21
  21.3 9.2 %psum.37 = f32[32]{0:T(128)S(1)} all-reduce(f32[32]{0:T(128)S(1)} %psum.36), channel_id=1, replica_groups=mesh['gx_0'=4,'gx_1'=2,'gx_2'=2,'gy_0'=4,'gy_1'=12] {'gx_2'}, use_global_device_ids=true, to_apply=%region_3.0 | all-reduce | flops 32 | bytes 256 | tf_op jit(solution)/shard_map/psum | solution.py:21
  30.5 20.1 %psum.38 = f32[32]{0:T(128)S(1)} all-reduce(f32[32]{0:T(128)S(1)} %psum.37), channel_id=1, replica_groups=mesh['gx_0'=4,'gx_1'=2,'gx_2'=2,'gy_0'=4,'gy_1'=12] {'gy_0'}, use_global_device_ids=true, to_apply=%region_4.0 | all-reduce | flops 32 | bytes 256 | tf_op jit(solution)/shard_map/psum | solution.py:21
  50.6 15.7 %psum.39 = f32[32]{0:T(128)S(1)} all-reduce(f32[32]{0:T(128)S(1)} %psum.38), channel_id=1, replica_groups=mesh['gx_0'=4,'gx_1'=2,'gx_2'=2,'gy_0'=4,'gy_1'=12] {'gy_1'}, use_global_device_ids=true, to_apply=%region_5.0 | all-reduce | flops 32 | bytes 256 | tf_op jit(solution)/shard_map/psum | solution.py:21
  66.4 2.8 %add_multiply_fusion = f32[4,33,8,128]{3,2,1,0:T(8,128)S(1)} fusion(f32[4,3,8,128]{3,2,1,0:T(8,128)S(1)} %reshape.41, f32[4,32,8,128]{3,2,1,0:T(8,128)S(1)} %slice.299, f32[4,3,8,128]{3,2,1,0:T(8,128)S(1)} %reshape.40, f32[33]{0:T(128)S(1)} %and_convert_fusion, f32[33,8,128]{2,1,0:T(8,128)S(1)} %minimum_bitcast_fusion.2, f32[33,8,128]{2,1,0:T(8,128)S(1)} %get-tuple-element.9), kind=kLoop, calls=%fused_computation.92 | loop fusion | flops 18112512 | bytes 1433732 | tf_op jit(solution)/shard_map/mul | solution.py:90
  69.2 0.1 pad.3.clone
  69.3 0.0 collective-permute-done
  69.3 0.3 copy.20
  69.6 0.0 collective-permute-done.1
  69.6 0.3 copy.22
  70.0 0.6 pad_maximum_fusion.1
  70.5 0.2 fusion.139
  70.7 0.1 copy.25
  70.8 9.9 %collective-permute-start.2 = (f32[5,32,3,134]{3,1,2,0:T(8,128)S(1)}, f32[5,32,3,134]{3,1,2,0:T(8,128)S(1)}, u32[]{:S(2)}, u32[]{:S(2)}) collective-permute-start(f32[5,32,3,134]{3,1,2,0:T(8,128)S(1)} %copy.25), channel_id=1, source_target_pairs={{0,48},{48,96},{96,144},{144,192},{192,240},{240,288},{288,336},{3... | collective-permute-start | bytes 771848 | tf_op jit(solution)/shard_map/ppermute | solution.py:30
  80.7 0.1 copy.27
  80.8 2.1 %collective-permute-start.3 = (f32[5,32,3,134]{3,1,2,0:T(8,128)S(1)}, f32[5,32,3,134]{3,1,2,0:T(8,128)S(1)}, u32[]{:S(2)}, u32[]{:S(2)}) collective-permute-start(f32[5,32,3,134]{3,1,2,0:T(8,128)S(1)} %copy.27), channel_id=1, source_target_pairs={{48,0},{96,48},{144,96},{192,144},{240,192},{288,240},{336,288},{3... | collective-permute-start | bytes 771848 | tf_op jit(solution)/shard_map/ppermute | solution.py:33
  82.9 0.2 maximum_bitcast_fusion.3
  83.1 3.3 %collective-permute-done.2 = f32[5,32,3,134]{3,1,2,0:T(8,128)S(1)} collective-permute-done((f32[5,32,3,134]{3,1,2,0:T(8,128)S(1)}, f32[5,32,3,134]{3,1,2,0:T(8,128)S(1)}, u32[]{:S(2)}, u32[]{:S(2)}) %collective-permute-start.2) | collective-permute-done | bytes 257312 | tf_op jit(solution)/shard_map/ppermute | solution.py:30
  86.5 0.3 copy.26
  86.8 5.5 %collective-permute-done.3 = f32[5,32,3,134]{3,1,2,0:T(8,128)S(1)} collective-permute-done((f32[5,32,3,134]{3,1,2,0:T(8,128)S(1)}, f32[5,32,3,134]{3,1,2,0:T(8,128)S(1)}, u32[]{:S(2)}, u32[]{:S(2)}) %collective-permute-start.3) | collective-permute-done | bytes 257312 | tf_op jit(solution)/shard_map/ppermute | solution.py:33
  92.3 0.3 copy.28
  92.6 0.5 fusion.95
  93.1 0.1 fusion.141
  93.2 0.1 slice.417
  93.3 0.5 maximum_bitcast_fusion.1
  93.8 1.2 %fusion.106 = f32[32,10,130]{2,1,0:T(8,128)S(1)} fusion(f32[32,14,134]{2,1,0:T(8,128)S(1)} %get-tuple-element.14, f32[32,14,134]{2,1,0:T(8,128)S(1)} %get-tuple-element.13), kind=kLoop, calls=%fused_computation.154 | loop fusion | flops 665600 | bytes 1497600 | tf_op jit(solution)/shard_map/mul | solution.py:101
  95.0 0.1 fusion.117
  95.2 0.2 fusion.116
  95.4 0.2 maximum_bitcast_fusion.2
  95.6 1.8 %maximum_maximum_fusion = (f32[5,32,11,134]{3,2,1,0:T(8,128)S(1)}, f32[5,32,11,134]{3,2,1,0:T(8,128)S(1)}) fusion(f32[5,32,8,3]{3,2,1,0:T(8,128)S(1)} %copy.22, f32[5,32,8,128]{3,2,1,0:T(8,128)S(1)} %copy-done, f32[5,32,8,3]{3,2,1,0:T(8,128)S(1)} %copy.20, f32[5,32,3,134]{3,2,1,0:T(4,128)S(1)} %copy.26, f32[5,32,3,134]{3,2,1,0:T(4,128)S(1)} %copy.28), kind=kLoop, calls=%fused_computation | loop fusion | flops 1415040 | bytes 3087360 | tf_op jit(solution)/shard_map/concatenate | solution.py:34
  97.4 0.0 copy-start.1
  97.4 0.0 copy-start.2
  97.4 0.0 copy-start.3
  97.4 5.5 %multiply_add_fusion.3 = (f32[4,32,8,129]{3,2,1,0:T(8,128)S(1)}, f32[4,32,8,129]{3,2,1,0:T(8,128)S(1)}) fusion(f32[5,32,8,3]{3,2,1,0:T(8,128)S(1)} %copy.22, f32[5,32,8,128]{3,2,1,0:T(8,128)S(1)} %copy-done, f32[5,32,8,3]{3,2,1,0:T(8,128)S(1)} %copy.20, f32[32,8,129]{2,1,0:T(8,128)S(1)} %minimum_bitcast_fusion.1, f32[32,8,129]{2,1,0:T(8,128)S(1)} %get-tuple-element.5, ...), kind=kLoop, calls=%fused_computation.47 | loop fusion | flops 17965056 | bytes 2139136 | tf_op jit(solution)/shard_map/add | solution.py:70
  102.9 0.1 fusion.135
  103.0 0.0 copy-done.1
  103.0 0.0 copy-done.2
  103.0 0.0 copy-done.3
  103.1 0.2 fusion.132
  103.3 5.7 %multiply_add_fusion = (f32[4,32,9,128]{3,2,1,0:T(8,128)S(1)}, f32[4,32,9,128]{3,2,1,0:T(8,128)S(1)}) fusion(f32[5,32,11,134]{3,2,1,0:T(8,128)S(1)} %get-tuple-element.18, f32[5,32,11,134]{3,2,1,0:T(8,128)S(1)} %get-tuple-element.17, f32[32,9,128]{2,1,0:T(8,128)S(1)} %minimum_bitcast_fusion, f32[32,9,128]{2,1,0:T(8,128)S(1)} %get-tuple-element.7, ...), kind=kLoop, calls=%fused_computation.19 | loop fusion | flops 19021824 | bytes 5160960 | tf_op jit(solution)/shard_map/add | solution.py:70
  109.0 1.3 %fusion.99 = f32[4,32,8,128]{3,2,1,0:T(8,128)} fusion(f32[4,32,9,128]{3,2,1,0:T(8,128)S(1)} %get-tuple-element.12, f32[4,32,8,129]{3,2,1,0:T(8,128)S(1)} %get-tuple-element.16, f32[4,33,8,128]{3,2,1,0:T(8,128)S(1)} %add_multiply_fusion, f32[4,32,9,128]{3,2,1,0:T(8,128)S(1)} %get-tuple-element.11, f32[4,32,8,129]{3,2,1,0:T(8,128)S(1)} %get-tuple-element.15, ...), kind=kLoop, calls=%fused_computation.144 | loop fusion | flops 2097152 | bytes 6684688 | tf_op jit(solution)/shard_map/add | solution.py:126
  (11 shorter events, 0.1 us)
Async XLA Ops:
  0.0 8.4 %copy-start = (f32[5,32,8,128]{3,2,1,0:T(8,128)S(1)}, f32[5,32,8,128]{3,2,1,0:T(8,128)}, u32[]{:S(2)}) copy-start(f32[5,32,8,128]{3,2,1,0:T(8,128)} %param.4) | copy-start | bytes 1966084
  1.9 67.4 %collective-permute-start = (f32[5,32,8,3]{1,2,3,0:T(8,128)S(1)}, f32[5,32,8,3]{1,2,3,0:T(8,128)S(1)}, u32[]{:S(2)}, u32[]{:S(2)}) collective-permute-start(f32[5,32,8,3]{1,2,3,0:T(8,128)S(1)} %copy.31), channel_id=1, source_target_pairs={{0,1},{1,2},{2,3},{3,4},{4,5},{5,6},{6,7},{7,8},{8,9},{9,10},{10,1... | collective-permute-start | bytes 46088 | tf_op jit(solution)/shard_map/ppermute | solution.py:30
  7.1 62.6 %collective-permute-start.1 = (f32[5,32,8,3]{1,2,3,0:T(8,128)S(1)}, f32[5,32,8,3]{1,2,3,0:T(8,128)S(1)}, u32[]{:S(2)}, u32[]{:S(2)}) collective-permute-start(f32[5,32,8,3]{1,2,3,0:T(8,128)S(1)} %copy.32), channel_id=1, source_target_pairs={{1,0},{2,1},{3,2},{4,3},{5,4},{6,5},{7,6},{8,7},{9,8},{10,9},{11,1... | collective-permute-start | bytes 46088 | tf_op jit(solution)/shard_map/ppermute | solution.py:33
  70.8 15.6 %collective-permute-start.2 = (f32[5,32,3,134]{3,1,2,0:T(8,128)S(1)}, f32[5,32,3,134]{3,1,2,0:T(8,128)S(1)}, u32[]{:S(2)}, u32[]{:S(2)}) collective-permute-start(f32[5,32,3,134]{3,1,2,0:T(8,128)S(1)} %copy.25), channel_id=1, source_target_pairs={{0,48},{48,96},{96,144},{144,192},{192,240},{240,288},{288,336},{3... | collective-permute-start | bytes 771848 | tf_op jit(solution)/shard_map/ppermute | solution.py:30
  80.8 11.5 %collective-permute-start.3 = (f32[5,32,3,134]{3,1,2,0:T(8,128)S(1)}, f32[5,32,3,134]{3,1,2,0:T(8,128)S(1)}, u32[]{:S(2)}, u32[]{:S(2)}) collective-permute-start(f32[5,32,3,134]{3,1,2,0:T(8,128)S(1)} %copy.27), channel_id=1, source_target_pairs={{48,0},{96,48},{144,96},{192,144},{240,192},{288,240},{336,288},{3... | collective-permute-start | bytes 771848 | tf_op jit(solution)/shard_map/ppermute | solution.py:33
  97.4 5.6 %copy-start.1 = (f32[8,128]{1,0:T(8,128)S(1)}, f32[8,128]{1,0:T(8,128)}, u32[]{:S(2)}) copy-start(f32[8,128]{1,0:T(8,128)} %param.6) | copy-start | bytes 12292
  97.4 5.6 %copy-start.2 = (f32[8,128]{1,0:T(8,128)S(1)}, f32[8,128]{1,0:T(8,128)}, u32[]{:S(2)}) copy-start(f32[8,128]{1,0:T(8,128)} %param.7) | copy-start | bytes 12292
  97.4 5.6 %copy-start.3 = (f32[8]{0:T(128)S(1)}, f32[8]{0:T(128)}, u32[]{:S(2)}) copy-start(f32[8]{0:T(128)} %param.5) | copy-start | bytes 100
where the time goes:
time: 111 us; the launch traced here: 110 us
  blocking collectives  57.6 us (52%)
  other arithmetic  21.2 us (19%)
  starting transfers between devices  18.1 us (16%)
  waiting for transfers between devices  8.83 us (8%)
  local copies, waits for them, and re-layouts  4.28 us (4%)
    psum x5, blocking collectives, one_axis_at_a_time(): x = lax.psum(x, axis)  57.6 us
    ppermute x2, starting transfers between devices, padded(): lax.ppermute(lax.slice_in_dim(block, block.shape[dim] - width, None, axis...  14.7 us
    add x2, other arithmetic, faces_along(): jnp.maximum(face_speed, 0.0) * low_side  11.2 us
    ppermute x2, waiting for transfers between devices, padded(): lax.ppermute(lax.slice_in_dim(block, 0, width, axis=dim), axis, backward)  5.48 us
    ppermute x2, starting transfers between devices, padded(): lax.ppermute(lax.slice_in_dim(block, 0, width, axis=dim), axis, backward)  3.39 us
    ppermute x2, waiting for transfers between devices, padded(): lax.ppermute(lax.slice_in_dim(block, block.shape[dim] - width, None, axis...  3.35 us
    mul x1, other arithmetic, section_update(): flux_z = flux_z * inside  2.81 us
    concatenate x2, other arithmetic, padded(): block = jnp.concatenate([low, block, high], axis=dim)  2.33 us
  transfers between devices with their start and end apart: 4, of which 2 were waited for; matrix products, arithmetic and copies ran while one was open for 4% of the time, Pallas kernels for 0%

commit v1 on v0

v1 whole, which is shorter than its diff:
```python
import functools

import jax
import jax.numpy as jnp
from jax import lax
from jax.experimental import pallas as pl
from jax.experimental.pallas import tpu as pltpu
from jax.sharding import Mesh
from jax.sharding import PartitionSpec as P

AXES = ("gx_0", "gx_1", "gx_2", "gy_0", "gy_1")
GX = ("gx_0", "gx_1", "gx_2")
GY = ("gy_0", "gy_1")
MESH = pl.DeviceIdType.MESH

WENO_EPS = 1e-06
SECTION_DT = 0.3
SMAG_COEF = 0.06
BACKGROUND = 0.05
BUOYANCY = 0.5

LANES = 128
ROWS = 8
EDGE = 24


def line_terms(q, sigma, size, upward, mixing):
    count = len(q) - 6
    g = [q[i + 1] - q[i] for i in range(count + 5)]
    bend = [g[i + 1] - g[i] for i in range(count + 4)]
    third = [bend[i + 1] - bend[i] for i in range(count + 3)]
    mid, low, high = [], [], []
    for i in range(count + 4):
        before, after, d = g[i], g[i + 1], bend[i]
        a = (d * (4.0 / 3.0)) * d + (before * after + WENO_EPS)
        d2 = d + d
        b = a + after * d2
        c = a - before * d2
        mid.append(a * a)
        low.append(b * b)
        high.append(c * c)
    out = []
    for f in range(count + 1):
        up = upward[f]
        e0 = jnp.where(up, low[f], high[f + 3])
        e1 = jnp.where(up, mid[f + 1], mid[f + 2])
        e2 = jnp.where(up, high[f + 2], low[f + 1])
        curve = jnp.where(up, bend[f + 1], bend[f + 2])
        t0 = jnp.where(up, third[f], third[f + 2])
        u = e0 * 3.0
        v = e2 + e2
        den = e1 * (e2 + u) + u * v
        num = e1 * (u * third[f + 1] + v * t0)
        flux = sigma[f] * ((q[f + 2] + q[f + 3]) - curve * (1.0 / 3.0)) + size[f] * (num / den)
        if mixing is not None:
            flux = flux + mixing[f] * g[f + 2]
        out.append(flux)
    return out


def speeds(s, keep_first=None, keep_last=None):
    count = len(s) - 6
    sigma = [(s[f + 2] + s[f + 3]) * (-0.25 * SECTION_DT) for f in range(count + 1)]
    if keep_first is not None:
        sigma[0] = jnp.where(keep_first, sigma[0], 0.0)
        sigma[count] = jnp.where(keep_last, sigma[count], 0.0)
    upward = [x < 0.0 for x in sigma]
    size = [jnp.abs(x) * (1.0 / 3.0) for x in sigma]
    return sigma, size, upward


def kernel(
    sizes, fields, coriolis, slope_east, slope_north, out,
    zf, xt, ysend, yrecv, halo, csend, crecv, eddy_y, eddy_z, eddy_v, eddy_x, xdiv, east, north, cor,
    row_send, recv_a, recv_z, recv_y,
    load_sem, send_a, got_a, send_z, got_z, send_y, got_y, send_h, got_h,
):
    nx, nl, nc, nh, nz = sizes
    ny = nh * nl
    n_gx, n_gy = nx * nl * nc, nh * nz
    depth = out.shape[1] // ROWS
    groups = depth // ROWS
    px, pl_, pc, ph, pz = (lax.axis_index(a) for a in AXES)
    py = ph * nl + pl_
    gx = (px * nl + pl_) * nc + pc
    gy = ph * nz + pz

    def at_gx(i):
        i = lax.rem(i + n_gx, n_gx)
        return (i // (nl * nc), lax.rem(i // nc, nl), lax.rem(i, nc), ph, pz)

    def at_gy(i):
        i = lax.rem(i + n_gy, n_gy)
        return (px, pl_, pc, i // nz, lax.rem(i, nz))

    peers_a = [
        (lax.rem(px + dx, nx), pl_, lax.rem(pc + dc, nc), ph, pz)
        for dx in range(nx)
        for dc in range(nc)
        if dx or dc
    ]
    peers_z = [(px, pl_, pc, ph, lax.rem(pz + dz, nz)) for dz in range(1, nz)]
    peers_y = []
    for dy in range(1, ny):
        y = lax.rem(py + dy, ny)
        peers_y.append((px, lax.rem(y, nl), pc, y // nl, pz))
    gx_low, gx_high = at_gx(gx - 1), at_gx(gx + 1)
    gy_low, gy_high = at_gy(gy - 1), at_gy(gy + 1)

    main = pl.ds(EDGE, depth * ROWS)
    loads = [
        pltpu.make_async_copy(fields.at[f], zf.at[f, main], load_sem.at[f]) for f in (3, 0, 1, 2, 4)
    ]
    loads.append(pltpu.make_async_copy(slope_east, east, load_sem.at[5]))
    loads.append(pltpu.make_async_copy(slope_north, north, load_sem.at[6]))
    loads.append(pltpu.make_async_copy(coriolis, cor, load_sem.at[7]))
    for copy in loads:
        copy.start()

    barrier = pltpu.get_barrier_semaphore()
    everyone = [*peers_a, *peers_z, *peers_y, gx_low, gx_high, gy_low, gy_high]
    for peer in everyone:
        pl.semaphore_signal(barrier, inc=1, device_id=peer, device_id_type=MESH)

    lane = lax.broadcasted_iota(jnp.int32, (ROWS, LANES), 1)
    sub = lax.broadcasted_iota(jnp.int32, (ROWS, LANES), 0)

    def strided(ref, f, first):
        return ref[f, pl.ds(first, ROWS, stride=ROWS), :]

    loads[0].wait()
    own = jnp.zeros((ROWS, LANES), jnp.float32)
    for g in range(groups):
        level = strided(zf, 3, EDGE + 64 * g)
        for j in range(1, ROWS):
            level = level + strided(zf, 3, EDGE + 64 * g + j)
        own = own + jnp.where(lane == sub + ROWS * g, jnp.sum(level, axis=1, keepdims=True), 0.0)
    own = jnp.sum(own, axis=0, keepdims=True)
    row_send[0] = own

    def remote(src, dst, send, got, peer):
        return pltpu.make_async_remote_copy(
            src_ref=src, dst_ref=dst, send_sem=send, recv_sem=got, device_id=peer, device_id_type=MESH
        )

    def phase(index, peers, dst, send, got):
        copies = [
            remote(row_send.at[index], dst.at[i], send.at[i], got.at[i], peer)
            for i, peer in enumerate(peers)
        ]
        for copy in copies:
            copy.start()
        return copies

    def total_of(copies, dst, value):
        for i, copy in enumerate(copies):
            copy.wait_recv()
        for i in range(len(copies)):
            value = value + dst[i]
        return value

    pl.semaphore_wait(barrier, len(everyone))
    first = phase(0, peers_a, recv_a, send_a, got_a)

    for copy in loads[1:]:
        copy.wait()

    for f in range(5):
        for r in range(3):
            slab = r * 4 + f
            if f == 4:
                if r:
                    continue
                slab = 12
            low_row, high_row = (r, 5 + r) if f < 4 else (0, 7)
            ysend[0, slab] = zf[f, pl.ds(EDGE + low_row, depth, stride=ROWS), :]
            ysend[1, slab] = zf[f, pl.ds(EDGE + high_row, depth, stride=ROWS), :]
        bottom = zf[f, pl.ds(EDGE, ROWS), :]
        top = zf[f, pl.ds(EDGE + (depth - 1) * ROWS, ROWS), :]
        for r in range(3):
            zf[f, pl.ds(r * ROWS, ROWS), :] = bottom
            zf[f, pl.ds(EDGE + (depth + r) * ROWS, ROWS), :] = top
    halves = depth * ROWS // LANES

    def turn(i, carry):
        f, half = i // halves, lax.rem(i, halves)
        block = zf[f, pl.ds(EDGE + half * LANES, LANES), :]
        xt[f, half, pl.ds(ROWS, LANES), :] = block.T
        return carry

    lax.fori_loop(0, 5 * halves, turn, 0)

    y_copies = [
        remote(ysend.at[0], yrecv.at[1], send_h.at[0], got_h.at[0], gx_low),
        remote(ysend.at[1], yrecv.at[0], send_h.at[1], got_h.at[1], gx_high),
    ]
    for copy in y_copies:
        copy.start()

    turning = jnp.zeros((ROWS, LANES), jnp.float32)
    for j in range(ROWS):
        turning = jnp.where(sub == j, cor[j] * SECTION_DT, turning)

    def upright(c, carry):
        base = c * ROWS * ROWS

        def cells(f, first=0, count=ROWS + 6):
            return [zf[f, pl.ds(base + (first + i) * ROWS, ROWS), :] for i in range(count)]

        p = cells(4, 2, ROWS + 2)
        slope = [(p[i + 2] - p[i]) * (0.5 * SECTION_DT) for i in range(ROWS)]
        top_factor = 1.0 - (c * ROWS).astype(jnp.float32) / depth
        w = cells(2)
        sigma, size, upward = speeds(w, c > 0, c < groups - 1)
        for f in range(4):
            q = w if f == 2 else cells(f)
            flux = line_terms(q, sigma, size, upward, None)
            for i in range(ROWS):
                value = q[i + 3] + (flux[i + 1] - flux[i])
                rows = pl.ds(base + i * ROWS, ROWS)
                if f == 0:
                    tilt = slope[i] * (top_factor - (i + 0.5) / depth)
                    value = value + east[...] * tilt + turning * zf[1, pl.ds(base + EDGE + i * ROWS, ROWS), :]
                elif f == 1:
                    tilt = slope[i] * (top_factor - (i + 0.5) / depth)
                    value = value + north[...] * tilt - turning * zf[0, pl.ds(base + EDGE + i * ROWS, ROWS), :]
                elif f == 2:
                    warm = zf[3, pl.ds(base + EDGE + i * ROWS, ROWS), :]
                    value = value - slope[i] + warm * (SECTION_DT * BUOYANCY)
                out[f, rows, :] = value
        return carry

    lax.fori_loop(0, groups, upright, 0)

    own = total_of(first, recv_a, own)
    row_send[1] = own
    x_copies = [
        remote(xt.at[:, :, pl.ds(ROWS, ROWS)], xt.at[:, :, pl.ds(ROWS + LANES, ROWS)], send_h.at[2], got_h.at[2], gy_low),
        remote(xt.at[:, :, pl.ds(LANES, ROWS)], xt.at[:, :, pl.ds(0, ROWS)], send_h.at[3], got_h.at[3], gy_high),
    ]
    second = phase(1, peers_z, recv_z, send_z, got_z)
    for copy in x_copies:
        copy.start()
    for copy in x_copies:
        copy.wait_recv()

    edge_rows = jnp.zeros((5, halves, ROWS, LANES), jnp.float32)

    @pl.when(gy == 0)
    def _():
        xt[:, :, pl.ds(0, ROWS), :] = edge_rows

    @pl.when(gy == n_gy - 1)
    def _():
        xt[:, :, pl.ds(ROWS + LANES, ROWS), :] = edge_rows

    gap = jnp.zeros((LANES - 2 * ROWS, LANES), jnp.float32)
    for f in range(2):
        for half in range(halves):
            block = jnp.concatenate(
                [xt[f, half, pl.ds(ROWS + LANES, ROWS), :], gap, xt[f, half, pl.ds(0, ROWS), :]], axis=0
            )
            halo[f, pl.ds(half * LANES, LANES), :] = block.T
    for f in range(2):
        csend[0, f] = halo[f, pl.ds(0, depth, stride=ROWS), :]
        csend[1, f] = halo[f, pl.ds(7, depth, stride=ROWS), :]

    own = total_of(second, recv_z, own)
    row_send[2] = own
    third = phase(2, peers_y, recv_y, send_y, got_y)
    c_copies = [
        remote(csend.at[0], crecv.at[1], send_h.at[4], got_h.at[4], gx_low),
        remote(csend.at[1], crecv.at[0], send_h.at[5], got_h.at[5], gx_high),
    ]
    for copy in c_copies:
        copy.start()
    for copy in y_copies + c_copies:
        copy.wait_recv()

    for side, at_edge in ((0, gx == 0), (1, gx == n_gx - 1)):

        @pl.when(at_edge)
        def _():
            yrecv[side] = jnp.zeros(yrecv.shape[1:], jnp.float32)
            crecv[side] = jnp.zeros(crecv.shape[1:], jnp.float32)

    def row(f, j, g):
        if j < 0:
            return yrecv[0, (j + 3) * 4 + f if f < 4 else 12, pl.ds(g * ROWS, ROWS), :]
        if j >= ROWS:
            return yrecv[1, (j - ROWS) * 4 + f if f < 4 else 12, pl.ds(g * ROWS, ROWS), :]
        return strided(zf, f, EDGE + g * 64 + j)

    def halo_row(f, j, g):
        if j < 0:
            return crecv[0, f, pl.ds(g * ROWS, ROWS), :]
        if j >= ROWS:
            return crecv[1, f, pl.ds(g * ROWS, ROWS), :]
        return strided(halo, f, g * 64 + j)

    def strength(ux, vx, uy, vy):
        cross = uy + vx
        return SMAG_COEF * jnp.sqrt(0.5 * (ux * ux + vy * vy) + 0.25 * (cross * cross) + BACKGROUND)

    def eddies(g, carry):
        u = [row(0, j, g) for j in range(-2, ROWS + 2)]
        v = [row(1, j, g) for j in range(-2, ROWS + 2)]
        hu = [halo_row(0, j, g) for j in range(-1, ROWS + 1)]
        hv = [halo_row(1, j, g) for j in range(-1, ROWS + 1)]
        left, right = lane == LANES - 1, lane == 0

        def across(inner, outer):
            plus = pltpu.roll(jnp.where(right, outer, inner), LANES - 1, 1)
            minus = pltpu.roll(jnp.where(left, outer, inner), 1, 1)
            return plus - minus

        for j in range(-1, ROWS + 1):
            ux, vx = across(u[j + 2], hu[j + 1]), across(v[j + 2], hv[j + 1])
            uy, vy = u[j + 3] - u[j + 1], v[j + 3] - v[j + 1]
            e = strength(ux, vx, uy, vy)
            eddy_y[j + 1, pl.ds(g * ROWS, ROWS), :] = e
            if 0 <= j < ROWS:
                eddy_z[pl.ds(g * 64 + j, ROWS, stride=ROWS), :] = e
                ux, vx = across(hu[j + 1], u[j + 2]), across(hv[j + 1], v[j + 2])
                uy, vy = hu[j + 2] - hu[j], hv[j + 2] - hv[j]
                eddy_v[pl.ds(g * 64 + j, ROWS, stride=ROWS), :] = strength(ux, vx, uy, vy)
        return carry

    lax.fori_loop(0, groups, eddies, 0)
    for half in range(halves):
        eddy_x[half, pl.ds(ROWS, LANES), :] = eddy_z[pl.ds(half * LANES, LANES), :].T
        outer = eddy_v[pl.ds(half * LANES, LANES), :].T
        eddy_x[half, pl.ds(0, ROWS), :] = outer[LANES - ROWS :]
        eddy_x[half, pl.ds(ROWS + LANES, ROWS), :] = outer[:ROWS]

    def northward(g, carry):
        v = [row(1, j, g) for j in range(-3, ROWS + 3)]
        sigma, size, upward = speeds(v)
        e = [eddy_y[j, pl.ds(g * ROWS, ROWS), :] for j in range(ROWS + 2)]
        mixing = [(e[f] + e[f + 1]) * (0.5 * SECTION_DT) for f in range(ROWS + 1)]
        p = [row(4, j, g) for j in range(-1, ROWS + 1)]
        for f in range(4):
            q = v if f == 1 else [row(f, j, g) for j in range(-3, ROWS + 3)]
            flux = line_terms(q, sigma, size, upward, mixing)
            for j in range(ROWS):
                value = flux[j + 1] - flux[j]
                if f == 1:
                    value = value - (p[j + 2] - p[j]) * (0.5 * SECTION_DT)
                rows = pl.ds(g * 64 + j, ROWS, stride=ROWS)
                out[f, rows, :] = out[f, rows, :] + value
        return carry

    lax.fori_loop(0, groups, northward, 0)

    step = LANES // ROWS

    def eastward(c, carry):
        half, start = c // 2, lax.rem(c, 2) * ROWS

        def cells(f, first=-3, count=ROWS + 6):
            return [
                xt[f, half, pl.ds(start + (ROWS + first + i), ROWS, stride=step), :] for i in range(count)
            ]

        u = cells(0)
        sigma, size, upward = speeds(u)
        e = [eddy_x[half, pl.ds(start + (ROWS - 1 + i), ROWS, stride=step), :] for i in range(ROWS + 2)]
        mixing = [(e[f] + e[f + 1]) * (0.5 * SECTION_DT) for f in range(ROWS + 1)]
        p = cells(4, -1, ROWS + 2)
        for f in range(4):
            q = u if f == 0 else cells(f)
            flux = line_terms(q, sigma, size, upward, mixing)
            for i in range(ROWS):
                value = flux[i + 1] - flux[i]
                if f == 0:
                    value = value - (p[i + 2] - p[i]) * (0.5 * SECTION_DT)
                xdiv[f, half, pl.ds(start + i, ROWS, stride=step), :] = value
        return carry

    lax.fori_loop(0, 2 * halves, eastward, 0)

    def turn_back(i, carry):
        f, half = i // halves, lax.rem(i, halves)
        rows = pl.ds(half * LANES, LANES)
        out[f, rows, :] = out[f, rows, :] + xdiv[f, half].T
        return carry

    lax.fori_loop(0, 4 * halves, turn_back, 0)

    own = total_of(third, recv_y, own)
    scale = SECTION_DT * BUOYANCY / (n_gx * ROWS * n_gy * LANES)
    for g in range(groups):
        mean = jnp.sum(jnp.where(lane == sub + ROWS * g, own * scale, 0.0), axis=1, keepdims=True)
        for j in range(ROWS):
            rows = pl.ds(g * 64 + j, ROWS, stride=ROWS)
            out[2, rows, :] = out[2, rows, :] - mean

    for copy in first + second + third + y_copies + x_copies + c_copies:
        copy.wait_send()


def body(sizes, fields, coriolis, slope_east, slope_north):
    depth = fields.shape[1]
    nx, nl, nc, nh, nz = sizes
    cells = depth * ROWS
    halves = cells // LANES
    f32 = jnp.float32
    any_space = pl.BlockSpec(memory_space=pl.ANY)
    count_a, count_z, count_y = max(nx * nc - 1, 1), max(nz - 1, 1), max(nl * nh - 1, 1)
    dma = pltpu.SemaphoreType.DMA
    out = pl.pallas_call(
        functools.partial(kernel, sizes),
        out_shape=jax.ShapeDtypeStruct((4, cells, LANES), f32),
        in_specs=[any_space] * 4,
        out_specs=pl.BlockSpec(memory_space=pltpu.VMEM),
        scratch_shapes=[
            pltpu.VMEM((5, cells + 2 * EDGE, LANES), f32),
            pltpu.VMEM((5, halves, LANES + 2 * ROWS, LANES), f32),
            pltpu.VMEM((2, 13, depth, LANES), f32),
            pltpu.VMEM((2, 13, depth, LANES), f32),
            pltpu.VMEM((2, cells, LANES), f32),
            pltpu.VMEM((2, 2, depth, LANES), f32),
            pltpu.VMEM((2, 2, depth, LANES), f32),
            pltpu.VMEM((ROWS + 2, depth, LANES), f32),
            pltpu.VMEM((cells, LANES), f32),
            pltpu.VMEM((cells, LANES), f32),
            pltpu.VMEM((halves, LANES + 2 * ROWS, LANES), f32),
            pltpu.VMEM((4, halves, LANES, LANES), f32),
            pltpu.VMEM((ROWS, LANES), f32),
            pltpu.VMEM((ROWS, LANES), f32),
            pltpu.SMEM((ROWS,), f32),
            pltpu.VMEM((3, 1, LANES), f32),
            pltpu.VMEM((count_a, 1, LANES), f32),
            pltpu.VMEM((count_z, 1, LANES), f32),
            pltpu.VMEM((count_y, 1, LANES), f32),
            dma((8,)),
            dma((count_a,)), dma((count_a,)),
            dma((count_z,)), dma((count_z,)),
            dma((count_y,)), dma((count_y,)),
            dma((6,)), dma((6,)),
        ],
        compiler_params=pltpu.CompilerParams(collective_id=0, has_side_effects=True),
    )(fields.reshape(5, cells, LANES), coriolis, slope_east, slope_north)
    return out.reshape(4, depth, ROWS, LANES)


def solution(mesh):
    return build(mesh, (4, 2, 2, 4, 12))


def build(mesh, sizes):
    finer = Mesh(mesh.devices.reshape(sizes), AXES)
    in_specs = (P(None, None, GX, GY), P(GX), P(GX, GY), P(GX, GY))
    out_specs = P(None, None, GX, GY)
    step = functools.partial(body, sizes)
    return jax.shard_map(step, mesh=finer, in_specs=in_specs, out_specs=out_specs, check_vma=False)
```

time: 111 us -> 39 us (0.35)
  blocking collectives: 57.6 us -> 0 us
  Pallas kernels: 0 us -> 37 us
  other arithmetic: 21.2 us -> 0 us
  starting transfers between devices: 18.1 us -> 0 us
  waiting for transfers between devices: 8.83 us -> 0 us
  local copies, waits for them, and re-layouts: 4.28 us -> 1.87 us
    psum x5 -> x0, blocking collectives: 57.6 us -> none  [one_axis_at_a_time(): x = lax.psum(x, axis)]
    pallas_call x0 -> x1, Pallas kernels: none -> 37 us  [body(): pl.pallas_call(functools.partial(kernel, sizes), out_shape=jax.ShapeDtype...]
    ppermute x4 -> x0, starting transfers between devices: 18.1 us -> none  [the longest x2 14.7 us: padded(): lax.ppermute(lax.slice_in_dim(block, block.shape[dim] - width, None, axis...]
    add x3 -> x0, other arithmetic: 12.4 us -> none  [the longest x2 11.2 us: faces_along(): jnp.maximum(face_speed, 0.0) * low_side]
    ppermute x4 -> x0, waiting for transfers between devices: 8.83 us -> none  [the longest x2 5.48 us: padded(): lax.ppermute(lax.slice_in_dim(block, 0, width, axis=dim), axis, backward)]
    mul x10 -> x0, other arithmetic: 4.84 us -> none  [the longest x1 2.81 us: section_update(): flux_z = flux_z * inside]
    concatenate x2 -> x0, other arithmetic: 2.33 us -> none  [padded(): block = jnp.concatenate([low, block, high], axis=dim)]
    slice x8 -> x0, local copies, waits for them, and re-layouts: 2.18 us -> none  [the longest x3 1.88 us: padded(): lax.slice_in_dim(block, block.shape[dim] - width, None, axis=dim)]
  transfers between devices with their start and end apart: 4 -> 0, of which waited for: 2 -> 0; matrix products, arithmetic and copies ran while one was open for 4% -> 0% of each run, Pallas kernels for 0% -> 0%
where the time goes in v1:
time: 39 us; the launch traced here: 38.8 us
  Pallas kernels  37 us (95%)
  local copies, waits for them, and re-layouts  1.87 us (5%)
    pallas_call x1, Pallas kernels, body(): pl.pallas_call(functools.partial(kernel, sizes), out_shape=jax.ShapeDtype...  37 us
    unnamed x1, local copies, waits for them, and re-layouts  1.87 us

profile of v1, /device:TPU:1, one launch (start us, length us, event | category | flops | bytes accessed | tf_op | source)
XLA Modules:
  0.0 38.8 jit_solution(17598344473627286928)
XLA Ops:
  0.0 37.0 %shard_map.46 = f32[4,256,128]{2,1,0:T(8,128)} custom-call(f32[5,256,128]{2,1,0:T(8,128)} %bitcast.3, f32[8]{0:T(128)} %coriolis.1, f32[8,128]{1,0:T(8,128)} %slope_east.1, f32[8,128]{1,0:T(8,128)} %slope_north.1), custom_call_target="tpu_custom_call" | custom-call | tf_op jit(solution)/shard_map/pallas_call | solution.py:411
  37.0 1.9 %copy.6 = f32[4,32,8,128]{3,2,1,0:T(8,128)} copy(f32[4,32,8,128]{3,2,1,0:T(8,128)} %bitcast.2) | data formatting | bytes 1048576

commit v2 on v1

--- a/solution.py
+++ b/solution.py
@@ -21,6 +21,7 @@
 
 LANES = 128
 ROWS = 8
+NEAR_Z, NEAR_Y = 3, 2
 EDGE = 24
 
 
@@ -73,7 +74,7 @@
     sizes, fields, coriolis, slope_east, slope_north, out,
     zf, xt, ysend, yrecv, halo, csend, crecv, eddy_y, eddy_z, eddy_v, eddy_x, xdiv, east, north, cor,
     row_send, recv_a, recv_z, recv_y,
-    load_sem, send_a, got_a, send_z, got_z, send_y, got_y, send_h, got_h,
+    load_sem, send_a, got_a, send_z, got_z, send_y, got_y, send_h, got_h, vouch,
 ):
     nx, nl, nc, nh, nz = sizes
     ny = nh * nl
@@ -99,11 +100,16 @@
         for dc in range(nc)
         if dx or dc
     ]
-    peers_z = [(px, pl_, pc, ph, lax.rem(pz + dz, nz)) for dz in range(1, nz)]
-    peers_y = []
-    for dy in range(1, ny):
+
+    def at_z(dz):
+        return (px, pl_, pc, ph, lax.rem(pz + dz, nz))
+
+    def at_y(dy):
         y = lax.rem(py + dy, ny)
-        peers_y.append((px, lax.rem(y, nl), pc, y // nl, pz))
+        return (px, lax.rem(y, nl), pc, y // nl, pz)
+
+    peers_z = [at_z(dz) for dz in range(1, nz)]
+    peers_y = [at_y(dy) for dy in range(1, ny)]
     gx_low, gx_high = at_gx(gx - 1), at_gx(gx + 1)
     gy_low, gy_high = at_gy(gy - 1), at_gy(gy + 1)
 
@@ -118,8 +124,10 @@
         copy.start()
 
     barrier = pltpu.get_barrier_semaphore()
-    everyone = [*peers_a, *peers_z, *peers_y, gx_low, gx_high, gy_low, gy_high]
-    for peer in everyone:
+    near_z = [at_z(d) for d in range(1, nz) if min(d, nz - d) <= NEAR_Z]
+    near_y = [at_y(d) for d in range(1, ny) if min(d, ny - d) <= NEAR_Y]
+    nearby = [*peers_a, *near_z, *near_y, gx_low, gx_high, gy_low, gy_high]
+    for peer in nearby:
         pl.semaphore_signal(barrier, inc=1, device_id=peer, device_id_type=MESH)
 
     lane = lax.broadcasted_iota(jnp.int32, (ROWS, LANES), 1)
@@ -159,8 +167,13 @@
             value = value + dst[i]
         return value
 
-    pl.semaphore_wait(barrier, len(everyone))
+    pl.semaphore_wait(barrier, len(nearby))
     first = phase(0, peers_a, recv_a, send_a, got_a)
+    relay_z = [at_z(NEAR_Z), at_z(nz - NEAR_Z)] if nz > 2 * NEAR_Z else []
+    relay_y = [at_y(NEAR_Y), at_y(ny - NEAR_Y)] if ny > 2 * NEAR_Y else []
+    for i, peers in enumerate((relay_z, relay_y)):
+        for peer in peers:
+            pl.semaphore_signal(vouch.at[i], inc=1, device_id=peer, device_id_type=MESH)
 
     for copy in loads[1:]:
         copy.wait()
@@ -194,7 +207,11 @@
         remote(ysend.at[0], yrecv.at[1], send_h.at[0], got_h.at[0], gx_low),
         remote(ysend.at[1], yrecv.at[0], send_h.at[1], got_h.at[1], gx_high),
     ]
-    for copy in y_copies:
+    x_copies = [
+        remote(xt.at[:, :, pl.ds(ROWS, ROWS)], xt.at[:, :, pl.ds(ROWS + LANES, ROWS)], send_h.at[2], got_h.at[2], gy_low),
+        remote(xt.at[:, :, pl.ds(LANES, ROWS)], xt.at[:, :, pl.ds(0, ROWS)], send_h.at[3], got_h.at[3], gy_high),
+    ]
+    for copy in x_copies + y_copies:
         copy.start()
 
     turning = jnp.zeros((ROWS, LANES), jnp.float32)
@@ -234,13 +251,9 @@
 
     own = total_of(first, recv_a, own)
     row_send[1] = own
-    x_copies = [
-        remote(xt.at[:, :, pl.ds(ROWS, ROWS)], xt.at[:, :, pl.ds(ROWS + LANES, ROWS)], send_h.at[2], got_h.at[2], gy_low),
-        remote(xt.at[:, :, pl.ds(LANES, ROWS)], xt.at[:, :, pl.ds(0, ROWS)], send_h.at[3], got_h.at[3], gy_high),
-    ]
+    if relay_z:
+        pl.semaphore_wait(vouch.at[0], 2)
     second = phase(1, peers_z, recv_z, send_z, got_z)
-    for copy in x_copies:
-        copy.start()
     for copy in x_copies:
         copy.wait_recv()
 
@@ -265,15 +278,17 @@
         csend[0, f] = halo[f, pl.ds(0, depth, stride=ROWS), :]
         csend[1, f] = halo[f, pl.ds(7, depth, stride=ROWS), :]
 
-    own = total_of(second, recv_z, own)
-    row_send[2] = own
-    third = phase(2, peers_y, recv_y, send_y, got_y)
     c_copies = [
         remote(csend.at[0], crecv.at[1], send_h.at[4], got_h.at[4], gx_low),
         remote(csend.at[1], crecv.at[0], send_h.at[5], got_h.at[5], gx_high),
     ]
     for copy in c_copies:
         copy.start()
+    own = total_of(second, recv_z, own)
+    row_send[2] = own
+    if relay_y:
+        pl.semaphore_wait(vouch.at[1], 2)
+    third = phase(2, peers_y, recv_y, send_y, got_y)
     for copy in y_copies + c_copies:
         copy.wait_recv()
 
@@ -405,13 +420,14 @@
     cells = depth * ROWS
     halves = cells // LANES
     f32 = jnp.float32
-    any_space = pl.BlockSpec(memory_space=pl.ANY)
+    hbm = pl.BlockSpec(memory_space=pltpu.HBM)
     count_a, count_z, count_y = max(nx * nc - 1, 1), max(nz - 1, 1), max(nl * nh - 1, 1)
     dma = pltpu.SemaphoreType.DMA
+    arrays = (fields.reshape(5, cells, LANES), coriolis, slope_east, slope_north)
     out = pl.pallas_call(
         functools.partial(kernel, sizes),
         out_shape=jax.ShapeDtypeStruct((4, cells, LANES), f32),
-        in_specs=[any_space] * 4,
+        in_specs=[hbm] * 4,
         out_specs=pl.BlockSpec(memory_space=pltpu.VMEM),
         scratch_shapes=[
             pltpu.VMEM((5, cells + 2 * EDGE, LANES), f32),
@@ -437,10 +453,12 @@
             dma((count_a,)), dma((count_a,)),
             dma((count_z,)), dma((count_z,)),
             dma((count_y,)), dma((count_y,)),
-            dma((6,)), dma((6,)),
+            dma((6,)), dma((6,)), pltpu.SemaphoreType.REGULAR((2,)),
         ],
-        compiler_params=pltpu.CompilerParams(collective_id=0, has_side_effects=True),
-    )(fields.reshape(5, cells, LANES), coriolis, slope_east, slope_north)
+        compiler_params=pltpu.CompilerParams(
+            collective_id=0, has_side_effects=True, vmem_limit_bytes=24 * 1024 * 1024
+        ),
+    )(*(pltpu.with_memory_space_constraint(a, pltpu.HBM) for a in arrays))
     return out.reshape(4, depth, ROWS, LANES)
 
 

time: 39 us -> 33 us (0.85)
  Pallas kernels: 37 us -> 31.9 us
  local copies, waits for them, and re-layouts: 1.87 us -> 0.8 us
    pallas_call x1, Pallas kernels: 37 us -> 31.9 us  [body(): pl.pallas_call(functools.partial(kernel, sizes), out_shape=jax.ShapeDtype...]
    unnamed x1, local copies, waits for them, and re-layouts: 1.87 us -> 0.8 us
where the time goes in v2:
time: 33 us; the launch traced here: 32.7 us
  Pallas kernels  31.9 us (97%)
  local copies, waits for them, and re-layouts  0.8 us (2%)
    pallas_call x1, Pallas kernels, body(): pl.pallas_call(functools.partial(kernel, sizes), out_shape=jax.ShapeDtype...  31.9 us
    unnamed x1, local copies, waits for them, and re-layouts  0.8 us

profile of v2, /device:TPU:1, one launch (start us, length us, event | category | flops | bytes accessed | tf_op | source)
XLA Modules:
  0.0 32.7 jit_solution(3409867788962219682)
XLA Ops:
  0.0 31.9 %shard_map.46 = f32[4,256,128]{2,1,0:T(8,128)S(1)} custom-call(f32[5,256,128]{2,1,0:T(8,128)} %bitcast.3, f32[8]{0:T(128)} %coriolis.1, f32[8,128]{1,0:T(8,128)} %slope_east.1, f32[8,128]{1,0:T(8,128)} %slope_north.1), custom_call_target="tpu_custom_call" | custom-call | tf_op jit(solution)/shard_map/pallas_call | solution.py:427
  31.9 0.8 %copy.6 = f32[4,32,8,128]{3,2,1,0:T(8,128)} copy(f32[4,32,8,128]{3,2,1,0:T(8,128)S(1)} %bitcast.2) | data formatting | bytes 1048576

commit v3 on v2

--- a/solution.py
+++ b/solution.py
@@ -83,36 +83,6 @@
     groups = depth // ROWS
     px, pl_, pc, ph, pz = (lax.axis_index(a) for a in AXES)
     py = ph * nl + pl_
-    gx = (px * nl + pl_) * nc + pc
-    gy = ph * nz + pz
-
-    def at_gx(i):
-        i = lax.rem(i + n_gx, n_gx)
-        return (i // (nl * nc), lax.rem(i // nc, nl), lax.rem(i, nc), ph, pz)
-
-    def at_gy(i):
-        i = lax.rem(i + n_gy, n_gy)
-        return (px, pl_, pc, i // nz, lax.rem(i, nz))
-
-    peers_a = [
-        (lax.rem(px + dx, nx), pl_, lax.rem(pc + dc, nc), ph, pz)
-        for dx in range(nx)
-        for dc in range(nc)
-        if dx or dc
-    ]
-
-    def at_z(dz):
-        return (px, pl_, pc, ph, lax.rem(pz + dz, nz))
-
-    def at_y(dy):
-        y = lax.rem(py + dy, ny)
-        return (px, lax.rem(y, nl), pc, y // nl, pz)
-
-    peers_z = [at_z(dz) for dz in range(1, nz)]
-    peers_y = [at_y(dy) for dy in range(1, ny)]
-    gx_low, gx_high = at_gx(gx - 1), at_gx(gx + 1)
-    gy_low, gy_high = at_gy(gy - 1), at_gy(gy + 1)
-
     main = pl.ds(EDGE, depth * ROWS)
     loads = [
         pltpu.make_async_copy(fields.at[f], zf.at[f, main], load_sem.at[f]) for f in (3, 0, 1, 2, 4)
@@ -123,6 +93,50 @@
     for copy in loads:
         copy.start()
 
+    gx = (px * nl + pl_) * nc + pc
+    gy = ph * nz + pz
+
+    def carry(coordinate, size):
+        over = coordinate >= size
+        return jnp.where(over, coordinate - size, coordinate), over.astype(jnp.int32)
+
+    def step_up(fast, sizes_fast):
+        carried, moved = 1, []
+        for coordinate, size in zip(fast, sizes_fast, strict=True):
+            coordinate, carried = carry(coordinate + carried, size)
+            moved.append(coordinate)
+        return moved
+
+    def step_down(fast, sizes_fast):
+        flipped = [size - 1 - c for c, size in zip(fast, sizes_fast, strict=True)]
+        return [size - 1 - c for c, size in zip(step_up(flipped, sizes_fast), sizes_fast, strict=True)]
+
+    def along_gx(step):
+        c, l, x = step((pc, pl_, px), (nc, nl, nx))
+        return (x, l, c, ph, pz)
+
+    def along_gy(step):
+        z, h = step((pz, ph), (nz, nh))
+        return (px, pl_, pc, h, z)
+
+    def at_z(dz):
+        return (px, pl_, pc, ph, carry(pz + dz, nz)[0])
+
+    def at_y(dy):
+        l, over = carry(pl_ + dy % nl, nl)
+        return (px, l, pc, carry(ph + dy // nl + over, nh)[0], pz)
+
+    peers_a = [
+        (carry(px + dx, nx)[0], pl_, carry(pc + dc, nc)[0], ph, pz)
+        for dx in range(nx)
+        for dc in range(nc)
+        if dx or dc
+    ]
+    peers_z = [at_z(dz) for dz in range(1, nz)]
+    peers_y = [at_y(dy) for dy in range(1, ny)]
+    gx_low, gx_high = along_gx(step_down), along_gx(step_up)
+    gy_low, gy_high = along_gy(step_down), along_gy(step_up)
+
     barrier = pltpu.get_barrier_semaphore()
     near_z = [at_z(d) for d in range(1, nz) if min(d, nz - d) <= NEAR_Z]
     near_y = [at_y(d) for d in range(1, ny) if min(d, ny - d) <= NEAR_Y]
@@ -166,14 +180,6 @@
         for i in range(len(copies)):
             value = value + dst[i]
         return value
-
-    pl.semaphore_wait(barrier, len(nearby))
-    first = phase(0, peers_a, recv_a, send_a, got_a)
-    relay_z = [at_z(NEAR_Z), at_z(nz - NEAR_Z)] if nz > 2 * NEAR_Z else []
-    relay_y = [at_y(NEAR_Y), at_y(ny - NEAR_Y)] if ny > 2 * NEAR_Y else []
-    for i, peers in enumerate((relay_z, relay_y)):
-        for peer in peers:
-            pl.semaphore_signal(vouch.at[i], inc=1, device_id=peer, device_id_type=MESH)
 
     for copy in loads[1:]:
         copy.wait()
@@ -195,21 +201,26 @@
             zf[f, pl.ds(EDGE + (depth + r) * ROWS, ROWS), :] = top
     halves = depth * ROWS // LANES
 
-    def turn(i, carry):
-        f, half = i // halves, lax.rem(i, halves)
-        block = zf[f, pl.ds(EDGE + half * LANES, LANES), :]
-        xt[f, half, pl.ds(ROWS, LANES), :] = block.T
-        return carry
-
-    lax.fori_loop(0, 5 * halves, turn, 0)
-
+    for f in range(5):
+        for half in range(halves):
+            block = zf[f, pl.ds(EDGE + half * LANES, LANES), :]
+            xt[f, half, pl.ds(ROWS, LANES), :] = block.T
+
+    pl.semaphore_wait(barrier, len(nearby))
+    first = phase(0, peers_a, recv_a, send_a, got_a)
+    relay_z = [at_z(NEAR_Z), at_z(nz - NEAR_Z)] if nz > 2 * NEAR_Z else []
+    relay_y = [at_y(NEAR_Y), at_y(ny - NEAR_Y)] if ny > 2 * NEAR_Y else []
+    for i, peers in enumerate((relay_z, relay_y)):
+        for peer in peers:
+            pl.semaphore_signal(vouch.at[i], inc=1, device_id=peer, device_id_type=MESH)
+
+    x_copies = [
+        remote(xt.at[:, :, pl.ds(ROWS, ROWS)], xt.at[:, :, pl.ds(ROWS + LANES, ROWS)], send_h.at[2], got_h.at[2], gy_low),
+        remote(xt.at[:, :, pl.ds(LANES, ROWS)], xt.at[:, :, pl.ds(0, ROWS)], send_h.at[3], got_h.at[3], gy_high),
+    ]
     y_copies = [
         remote(ysend.at[0], yrecv.at[1], send_h.at[0], got_h.at[0], gx_low),
         remote(ysend.at[1], yrecv.at[0], send_h.at[1], got_h.at[1], gx_high),
-    ]
-    x_copies = [
-        remote(xt.at[:, :, pl.ds(ROWS, ROWS)], xt.at[:, :, pl.ds(ROWS + LANES, ROWS)], send_h.at[2], got_h.at[2], gy_low),
-        remote(xt.at[:, :, pl.ds(LANES, ROWS)], xt.at[:, :, pl.ds(0, ROWS)], send_h.at[3], got_h.at[3], gy_high),
     ]
     for copy in x_copies + y_copies:
         copy.start()
@@ -394,13 +405,10 @@
 
     lax.fori_loop(0, 2 * halves, eastward, 0)
 
-    def turn_back(i, carry):
-        f, half = i // halves, lax.rem(i, halves)
-        rows = pl.ds(half * LANES, LANES)
-        out[f, rows, :] = out[f, rows, :] + xdiv[f, half].T
-        return carry
-
-    lax.fori_loop(0, 4 * halves, turn_back, 0)
+    for f in range(4):
+        for half in range(halves):
+            rows = pl.ds(half * LANES, LANES)
+            out[f, rows, :] = out[f, rows, :] + xdiv[f, half].T
 
     own = total_of(third, recv_y, own)
     scale = SECTION_DT * BUOYANCY / (n_gx * ROWS * n_gy * LANES)

time: 33 us -> 32.9 us (level)
  no operation moved by 1% of the time
where the time goes in v3:
time: 32.9 us; the launch traced here: 32.7 us
  Pallas kernels  31.9 us (97%)
  local copies, waits for them, and re-layouts  0.8 us (2%)
    pallas_call x1, Pallas kernels, body(): pl.pallas_call(functools.partial(kernel, sizes), out_shape=jax.ShapeDtype...  31.9 us
    unnamed x1, local copies, waits for them, and re-layouts  0.8 us

profile of v3, /device:TPU:1, one launch (start us, length us, event | category | flops | bytes accessed | tf_op | source)
XLA Modules:
  0.0 32.7 jit_solution(1316029991956052036)
XLA Ops:
  0.0 31.9 %shard_map.46 = f32[4,256,128]{2,1,0:T(8,128)S(1)} custom-call(f32[5,256,128]{2,1,0:T(8,128)} %bitcast.3, f32[8]{0:T(128)} %coriolis.1, f32[8,128]{1,0:T(8,128)} %slope_east.1, f32[8,128]{1,0:T(8,128)} %slope_north.1), custom_call_target="tpu_custom_call" | custom-call | tf_op jit(solution)/shard_map/pallas_call | solution.py:435
  31.9 0.8 %copy.6 = f32[4,32,8,128]{3,2,1,0:T(8,128)} copy(f32[4,32,8,128]{3,2,1,0:T(8,128)S(1)} %bitcast.2) | data formatting | bytes 1048576

commit v4 on v3

--- a/solution.py
+++ b/solution.py
@@ -21,11 +21,11 @@
 
 LANES = 128
 ROWS = 8
-NEAR_Z, NEAR_Y = 3, 2
+NEAR_Y = 2
 EDGE = 24
 
 
-def line_terms(q, sigma, size, upward, mixing):
+def line_terms(q, sigma, size, upward):
     count = len(q) - 6
     g = [q[i + 1] - q[i] for i in range(count + 5)]
     bend = [g[i + 1] - g[i] for i in range(count + 4)]
@@ -53,8 +53,6 @@
         den = e1 * (e2 + u) + u * v
         num = e1 * (u * third[f + 1] + v * t0)
         flux = sigma[f] * ((q[f + 2] + q[f + 3]) - curve * (1.0 / 3.0)) + size[f] * (num / den)
-        if mixing is not None:
-            flux = flux + mixing[f] * g[f + 2]
         out.append(flux)
     return out
 
@@ -73,7 +71,7 @@
 def kernel(
     sizes, fields, coriolis, slope_east, slope_north, out,
     zf, xt, ysend, yrecv, halo, csend, crecv, eddy_y, eddy_z, eddy_v, eddy_x, xdiv, east, north, cor,
-    row_send, recv_a, recv_z, recv_y,
+    recv_a, recv_z, recv_y,
     load_sem, send_a, got_a, send_z, got_z, send_y, got_y, send_h, got_h, vouch,
 ):
     nx, nl, nc, nh, nz = sizes
@@ -84,12 +82,15 @@
     px, pl_, pc, ph, pz = (lax.axis_index(a) for a in AXES)
     py = ph * nl + pl_
     main = pl.ds(EDGE, depth * ROWS)
+    winds = pl.ds(0, 3)
     loads = [
-        pltpu.make_async_copy(fields.at[f], zf.at[f, main], load_sem.at[f]) for f in (3, 0, 1, 2, 4)
+        pltpu.make_async_copy(fields.at[3], zf.at[3, main], load_sem.at[0]),
+        pltpu.make_async_copy(fields.at[winds], zf.at[winds, main], load_sem.at[1]),
+        pltpu.make_async_copy(fields.at[4], zf.at[4, main], load_sem.at[2]),
+        pltpu.make_async_copy(slope_east, east, load_sem.at[3]),
+        pltpu.make_async_copy(slope_north, north, load_sem.at[4]),
+        pltpu.make_async_copy(coriolis, cor, load_sem.at[5]),
     ]
-    loads.append(pltpu.make_async_copy(slope_east, east, load_sem.at[5]))
-    loads.append(pltpu.make_async_copy(slope_north, north, load_sem.at[6]))
-    loads.append(pltpu.make_async_copy(coriolis, cor, load_sem.at[7]))
     for copy in loads:
         copy.start()
 
@@ -119,30 +120,46 @@
         z, h = step((pz, ph), (nz, nh))
         return (px, pl_, pc, h, z)
 
-    def at_z(dz):
-        return (px, pl_, pc, ph, carry(pz + dz, nz)[0])
-
-    def at_y(dy):
-        l, over = carry(pl_ + dy % nl, nl)
-        return (px, l, pc, carry(ph + dy // nl + over, nh)[0], pz)
-
-    peers_a = [
-        (carry(px + dx, nx)[0], pl_, carry(pc + dc, nc)[0], ph, pz)
-        for dx in range(nx)
-        for dc in range(nc)
-        if dx or dc
-    ]
-    peers_z = [at_z(dz) for dz in range(1, nz)]
-    peers_y = [at_y(dy) for dy in range(1, ny)]
+    def at_a(i):
+        x = lax.div(i, nc)
+        return (x, pl_, i - x * nc, ph, pz)
+
+    def at_z(i):
+        return (px, pl_, pc, ph, i)
+
+    def at_y(i):
+        h = lax.div(i, nl)
+        return (px, i - h * nl, pc, h, pz)
+
+    n_a = nx * nc
+    pa, py = px * nc + pc, ph * nl + pl_
+    near_y = [carry(py + d, ny)[0] for d in range(1, ny) if min(d, ny - d) <= NEAR_Y]
     gx_low, gx_high = along_gx(step_down), along_gx(step_up)
     gy_low, gy_high = along_gy(step_down), along_gy(step_up)
 
     barrier = pltpu.get_barrier_semaphore()
-    near_z = [at_z(d) for d in range(1, nz) if min(d, nz - d) <= NEAR_Z]
-    near_y = [at_y(d) for d in range(1, ny) if min(d, ny - d) <= NEAR_Y]
-    nearby = [*peers_a, *near_z, *near_y, gx_low, gx_high, gy_low, gy_high]
-    for peer in nearby:
-        pl.semaphore_signal(barrier, inc=1, device_id=peer, device_id_type=MESH)
+
+    def one(condition):
+        return condition.astype(jnp.int32)
+
+    def each(first, last, visit):
+        def step(i, unused):
+            visit(i)
+            return unused
+
+        lax.fori_loop(first, last, step, 0)
+
+    def tell(sem, peer):
+        pl.semaphore_signal(sem, inc=1, device_id=peer, device_id_type=MESH)
+
+    together = [at_y(y) for y in near_y] + [gx_low, gx_high]
+    for peer in together:
+        tell(barrier, peer)
+    for i in range(1, n_a):
+        tell(barrier, at_a(carry(pa + i, n_a)[0]))
+    each(pz + 1, nz, lambda i: tell(barrier, at_z(i)))
+    pl.when(pz == 0)(functools.partial(tell, barrier, gy_low))
+    expected = len(together) + n_a - 1 + pz + one(pz == nz - 1)
 
     lane = lax.broadcasted_iota(jnp.int32, (ROWS, LANES), 1)
     sub = lax.broadcasted_iota(jnp.int32, (ROWS, LANES), 0)
@@ -158,27 +175,27 @@
             level = level + strided(zf, 3, EDGE + 64 * g + j)
         own = own + jnp.where(lane == sub + ROWS * g, jnp.sum(level, axis=1, keepdims=True), 0.0)
     own = jnp.sum(own, axis=0, keepdims=True)
-    row_send[0] = own
+    recv_a[pa] = own
 
     def remote(src, dst, send, got, peer):
         return pltpu.make_async_remote_copy(
             src_ref=src, dst_ref=dst, send_sem=send, recv_sem=got, device_id=peer, device_id_type=MESH
         )
 
-    def phase(index, peers, dst, send, got):
-        copies = [
-            remote(row_send.at[index], dst.at[i], send.at[i], got.at[i], peer)
-            for i, peer in enumerate(peers)
-        ]
-        for copy in copies:
-            copy.start()
-        return copies
-
-    def total_of(copies, dst, value):
-        for i, copy in enumerate(copies):
-            copy.wait_recv()
-        for i in range(len(copies)):
-            value = value + dst[i]
+    def send_row(rows, me, send, got, place):
+        return lambda i: remote(rows.at[me], rows.at[me], send, got, place(i)).start()
+
+    def others(rows):
+        return rows.at[pl.ds(0, rows.shape[0] - 1)]
+
+    def all_of(ref, sem):
+        pltpu.make_async_copy(ref, ref, sem).wait()
+
+    def total_of(rows, got):
+        all_of(others(rows), got)
+        value = rows[0]
+        for i in range(1, rows.shape[0]):
+            value = value + rows[i]
         return value
 
     for copy in loads[1:]:
@@ -206,24 +223,27 @@
             block = zf[f, pl.ds(EDGE + half * LANES, LANES), :]
             xt[f, half, pl.ds(ROWS, LANES), :] = block.T
 
-    pl.semaphore_wait(barrier, len(nearby))
-    first = phase(0, peers_a, recv_a, send_a, got_a)
-    relay_z = [at_z(NEAR_Z), at_z(nz - NEAR_Z)] if nz > 2 * NEAR_Z else []
-    relay_y = [at_y(NEAR_Y), at_y(ny - NEAR_Y)] if ny > 2 * NEAR_Y else []
-    for i, peers in enumerate((relay_z, relay_y)):
-        for peer in peers:
-            pl.semaphore_signal(vouch.at[i], inc=1, device_id=peer, device_id_type=MESH)
-
+    pl.semaphore_wait(barrier, expected)
+    to_a = send_row(recv_a, pa, send_a, got_a, at_a)
+    for i in range(1, n_a):
+        to_a(carry(pa + i, n_a)[0])
+    tile_low, tile_high = xt.at[:, :, pl.ds(ROWS, ROWS)], xt.at[:, :, pl.ds(LANES, ROWS)]
+    past_low, past_high = xt.at[:, :, pl.ds(0, ROWS)], xt.at[:, :, pl.ds(ROWS + LANES, ROWS)]
     x_copies = [
-        remote(xt.at[:, :, pl.ds(ROWS, ROWS)], xt.at[:, :, pl.ds(ROWS + LANES, ROWS)], send_h.at[2], got_h.at[2], gy_low),
-        remote(xt.at[:, :, pl.ds(LANES, ROWS)], xt.at[:, :, pl.ds(0, ROWS)], send_h.at[3], got_h.at[3], gy_high),
+        remote(tile_low, past_high, send_h.at[2], got_h.at[2], gy_low),
+        remote(tile_high, past_low, send_h.at[3], got_h.at[3], gy_high),
     ]
-    y_copies = [
-        remote(ysend.at[0], yrecv.at[1], send_h.at[0], got_h.at[0], gx_low),
-        remote(ysend.at[1], yrecv.at[0], send_h.at[1], got_h.at[1], gx_high),
-    ]
-    for copy in x_copies + y_copies:
-        copy.start()
+    pl.when(pz == nz - 1)(x_copies[1].start)
+    pl.when(pz > 0)(x_copies[0].start)
+    remote(ysend.at[0], yrecv.at[1], send_h.at[0], got_h.at[0], gx_low).start()
+    remote(ysend.at[1], yrecv.at[0], send_h.at[0], got_h.at[0], gx_high).start()
+    pl.when(pz == nz - 1)(functools.partial(tell, vouch.at[1], gy_high))
+    pl.when(pz > 0)(functools.partial(tell, vouch.at[0], gy_low))
+    each(0, pz, lambda i: tell(vouch.at[2], at_z(i)))
+    far_y = ny > 2 * NEAR_Y
+    if far_y:
+        for d in (NEAR_Y, ny - NEAR_Y):
+            tell(vouch.at[3], at_y(carry(py + d, ny)[0]))
 
     turning = jnp.zeros((ROWS, LANES), jnp.float32)
     for j in range(ROWS):
@@ -242,7 +262,7 @@
         sigma, size, upward = speeds(w, c > 0, c < groups - 1)
         for f in range(4):
             q = w if f == 2 else cells(f)
-            flux = line_terms(q, sigma, size, upward, None)
+            flux = line_terms(q, sigma, size, upward)
             for i in range(ROWS):
                 value = q[i + 3] + (flux[i + 1] - flux[i])
                 rows = pl.ds(base + i * ROWS, ROWS)
@@ -260,11 +280,25 @@
 
     lax.fori_loop(0, groups, upright, 0)
 
-    own = total_of(first, recv_a, own)
-    row_send[1] = own
-    if relay_z:
-        pl.semaphore_wait(vouch.at[0], 2)
-    second = phase(1, peers_z, recv_z, send_z, got_z)
+    recv_z[pz] = total_of(recv_a, got_a)
+    to_z = send_row(recv_z, pz, send_z, got_z, at_z)
+    each(0, pz, to_z)
+
+    @pl.when(pz < nz - 1)
+    def _():
+        pl.semaphore_wait(vouch.at[0], 1)
+        x_copies[1].start()
+
+    @pl.when(pz < nz - 1)
+    def _():
+        pl.semaphore_wait(vouch.at[2], nz - 1 - pz)
+        each(pz + 1, nz, to_z)
+
+    @pl.when(pz == 0)
+    def _():
+        pl.semaphore_wait(vouch.at[1], 1)
+        x_copies[0].start()
+
     for copy in x_copies:
         copy.wait_recv()
 
@@ -289,26 +323,39 @@
         csend[0, f] = halo[f, pl.ds(0, depth, stride=ROWS), :]
         csend[1, f] = halo[f, pl.ds(7, depth, stride=ROWS), :]
 
-    c_copies = [
-        remote(csend.at[0], crecv.at[1], send_h.at[4], got_h.at[4], gx_low),
-        remote(csend.at[1], crecv.at[0], send_h.at[5], got_h.at[5], gx_high),
-    ]
-    for copy in c_copies:
-        copy.start()
-    own = total_of(second, recv_z, own)
-    row_send[2] = own
-    if relay_y:
-        pl.semaphore_wait(vouch.at[1], 2)
-    third = phase(2, peers_y, recv_y, send_y, got_y)
-    for copy in y_copies + c_copies:
-        copy.wait_recv()
-
+    remote(csend.at[0], crecv.at[1], send_h.at[1], got_h.at[1], gx_low).start()
+    remote(csend.at[1], crecv.at[0], send_h.at[1], got_h.at[1], gx_high).start()
+    step = LANES // ROWS
+
+    def eastward(c, carry):
+        half, start = c // 2, lax.rem(c, 2) * ROWS
+
+        def cells(f, first=-3, count=ROWS + 6):
+            return [
+                xt[f, half, pl.ds(start + (ROWS + first + i), ROWS, stride=step), :] for i in range(count)
+            ]
+
+        u = cells(0)
+        sigma, size, upward = speeds(u)
+        p = cells(4, -1, ROWS + 2)
+        for f in range(4):
+            q = u if f == 0 else cells(f)
+            flux = line_terms(q, sigma, size, upward)
+            for i in range(ROWS):
+                value = flux[i + 1] - flux[i]
+                if f == 0:
+                    value = value - (p[i + 2] - p[i]) * (0.5 * SECTION_DT)
+                xdiv[f, half, pl.ds(start + i, ROWS, stride=step), :] = value
+        return carry
+
+    lax.fori_loop(0, 2 * halves, eastward, 0)
+
+    all_of(yrecv, got_h.at[0])
     for side, at_edge in ((0, gx == 0), (1, gx == n_gx - 1)):
 
         @pl.when(at_edge)
         def _():
             yrecv[side] = jnp.zeros(yrecv.shape[1:], jnp.float32)
-            crecv[side] = jnp.zeros(crecv.shape[1:], jnp.float32)
 
     def row(f, j, g):
         if j < 0:
@@ -327,6 +374,37 @@
     def strength(ux, vx, uy, vy):
         cross = uy + vx
         return SMAG_COEF * jnp.sqrt(0.5 * (ux * ux + vy * vy) + 0.25 * (cross * cross) + BACKGROUND)
+
+    def northward(g, carry):
+        v = [row(1, j, g) for j in range(-3, ROWS + 3)]
+        sigma, size, upward = speeds(v)
+        p = [row(4, j, g) for j in range(-1, ROWS + 1)]
+        for f in range(4):
+            q = v if f == 1 else [row(f, j, g) for j in range(-3, ROWS + 3)]
+            flux = line_terms(q, sigma, size, upward)
+            for j in range(ROWS):
+                value = flux[j + 1] - flux[j]
+                if f == 1:
+                    value = value - (p[j + 2] - p[j]) * (0.5 * SECTION_DT)
+                rows = pl.ds(g * 64 + j, ROWS, stride=ROWS)
+                out[f, rows, :] = out[f, rows, :] + value
+        return carry
+
+    lax.fori_loop(0, groups, northward, 0)
+
+    recv_y[py] = total_of(recv_z, got_z)
+    if far_y:
+        pl.semaphore_wait(vouch.at[3], 2)
+    to_y = send_row(recv_y, py, send_y, got_y, at_y)
+    for i in range(1, ny):
+        to_y(carry(py + i, ny)[0])
+
+    all_of(crecv, got_h.at[1])
+    for side, at_edge in ((0, gx == 0), (1, gx == n_gx - 1)):
+
+        @pl.when(at_edge)
+        def _():
+            crecv[side] = jnp.zeros(crecv.shape[1:], jnp.float32)
 
     def eddies(g, carry):
         u = [row(0, j, g) for j in range(-2, ROWS + 2)]
@@ -359,58 +437,47 @@
         eddy_x[half, pl.ds(0, ROWS), :] = outer[LANES - ROWS :]
         eddy_x[half, pl.ds(ROWS + LANES, ROWS), :] = outer[:ROWS]
 
-    def northward(g, carry):
-        v = [row(1, j, g) for j in range(-3, ROWS + 3)]
-        sigma, size, upward = speeds(v)
+    def mix(e, q, add):
+        count = len(e) - 2
+        half_sum = [(e[i] + e[i + 1]) * (0.5 * SECTION_DT) for i in range(count + 1)]
+        for f in range(4):
+            line = q(f)
+            flux = [half_sum[i] * (line[i + 1] - line[i]) for i in range(count + 1)]
+            for i in range(count):
+                add(f, i, flux[i + 1] - flux[i])
+
+    def mix_north(g, carry):
+        def add(f, j, value):
+            rows = pl.ds(g * 64 + j, ROWS, stride=ROWS)
+            out[f, rows, :] = out[f, rows, :] + value
+
         e = [eddy_y[j, pl.ds(g * ROWS, ROWS), :] for j in range(ROWS + 2)]
-        mixing = [(e[f] + e[f + 1]) * (0.5 * SECTION_DT) for f in range(ROWS + 1)]
-        p = [row(4, j, g) for j in range(-1, ROWS + 1)]
-        for f in range(4):
-            q = v if f == 1 else [row(f, j, g) for j in range(-3, ROWS + 3)]
-            flux = line_terms(q, sigma, size, upward, mixing)
-            for j in range(ROWS):
-                value = flux[j + 1] - flux[j]
-                if f == 1:
-                    value = value - (p[j + 2] - p[j]) * (0.5 * SECTION_DT)
-                rows = pl.ds(g * 64 + j, ROWS, stride=ROWS)
-                out[f, rows, :] = out[f, rows, :] + value
+        mix(e, lambda f: [row(f, j, g) for j in range(-1, ROWS + 1)], add)
         return carry
 
-    lax.fori_loop(0, groups, northward, 0)
-
-    step = LANES // ROWS
-
-    def eastward(c, carry):
+    lax.fori_loop(0, groups, mix_north, 0)
+
+    def mix_east(c, carry):
         half, start = c // 2, lax.rem(c, 2) * ROWS
 
-        def cells(f, first=-3, count=ROWS + 6):
-            return [
-                xt[f, half, pl.ds(start + (ROWS + first + i), ROWS, stride=step), :] for i in range(count)
-            ]
-
-        u = cells(0)
-        sigma, size, upward = speeds(u)
-        e = [eddy_x[half, pl.ds(start + (ROWS - 1 + i), ROWS, stride=step), :] for i in range(ROWS + 2)]
-        mixing = [(e[f] + e[f + 1]) * (0.5 * SECTION_DT) for f in range(ROWS + 1)]
-        p = cells(4, -1, ROWS + 2)
-        for f in range(4):
-            q = u if f == 0 else cells(f)
-            flux = line_terms(q, sigma, size, upward, mixing)
-            for i in range(ROWS):
-                value = flux[i + 1] - flux[i]
-                if f == 0:
-                    value = value - (p[i + 2] - p[i]) * (0.5 * SECTION_DT)
-                xdiv[f, half, pl.ds(start + i, ROWS, stride=step), :] = value
+        def line(ref, *lead):
+            return [ref[*lead, half, pl.ds(start + (ROWS - 1 + i), ROWS, stride=step), :] for i in range(ROWS + 2)]
+
+        def add(f, i, value):
+            rows = pl.ds(start + i, ROWS, stride=step)
+            xdiv[f, half, rows, :] = xdiv[f, half, rows, :] + value
+
+        mix(line(eddy_x), lambda f: line(xt, f), add)
         return carry
 
-    lax.fori_loop(0, 2 * halves, eastward, 0)
+    lax.fori_loop(0, 2 * halves, mix_east, 0)
 
     for f in range(4):
         for half in range(halves):
             rows = pl.ds(half * LANES, LANES)
             out[f, rows, :] = out[f, rows, :] + xdiv[f, half].T
 
-    own = total_of(third, recv_y, own)
+    own = total_of(recv_y, got_y)
     scale = SECTION_DT * BUOYANCY / (n_gx * ROWS * n_gy * LANES)
     for g in range(groups):
         mean = jnp.sum(jnp.where(lane == sub + ROWS * g, own * scale, 0.0), axis=1, keepdims=True)
@@ -418,7 +485,15 @@
             rows = pl.ds(g * 64 + j, ROWS, stride=ROWS)
             out[2, rows, :] = out[2, rows, :] - mean
 
-    for copy in first + second + third + y_copies + x_copies + c_copies:
+    for ref, sem in (
+        (others(recv_a), send_a),
+        (others(recv_z), send_z),
+        (others(recv_y), send_y),
+        (ysend, send_h.at[0]),
+        (csend, send_h.at[1]),
+    ):
+        all_of(ref, sem)
+    for copy in x_copies:
         copy.wait_send()
 
 
@@ -429,7 +504,6 @@
     halves = cells // LANES
     f32 = jnp.float32
     hbm = pl.BlockSpec(memory_space=pltpu.HBM)
-    count_a, count_z, count_y = max(nx * nc - 1, 1), max(nz - 1, 1), max(nl * nh - 1, 1)
     dma = pltpu.SemaphoreType.DMA
     arrays = (fields.reshape(5, cells, LANES), coriolis, slope_east, slope_north)
     out = pl.pallas_call(
@@ -453,15 +527,11 @@
             pltpu.VMEM((ROWS, LANES), f32),
             pltpu.VMEM((ROWS, LANES), f32),
             pltpu.SMEM((ROWS,), f32),
-            pltpu.VMEM((3, 1, LANES), f32),
-            pltpu.VMEM((count_a, 1, LANES), f32),
-            pltpu.VMEM((count_z, 1, LANES), f32),
-            pltpu.VMEM((count_y, 1, LANES), f32),
-            dma((8,)),
-            dma((count_a,)), dma((count_a,)),
-            dma((count_z,)), dma((count_z,)),
-            dma((count_y,)), dma((count_y,)),
-            dma((6,)), dma((6,)), pltpu.SemaphoreType.REGULAR((2,)),
+            pltpu.VMEM((nx * nc, 1, LANES), f32),
+            pltpu.VMEM((nz, 1, LANES), f32),
+            pltpu.VMEM((nl * nh, 1, LANES), f32),
+            dma((6,)), dma, dma, dma, dma, dma, dma, dma((4,)), dma((4,)),
+            pltpu.SemaphoreType.REGULAR((4,)),
         ],
         compiler_params=pltpu.CompilerParams(
             collective_id=0, has_side_effects=True, vmem_limit_bytes=24 * 1024 * 1024

time: 32.9 us -> 30.2 us (0.918)
  Pallas kernels: 31.9 us -> 29.2 us
    pallas_call x1, Pallas kernels: 31.9 us -> 29.2 us  [body(): pl.pallas_call(functools.partial(kernel, sizes), out_shape=jax.ShapeDtype...]
where the time goes in v4:
time: 30.2 us; the launch traced here: 30 us
  Pallas kernels  29.2 us (97%)
  local copies, waits for them, and re-layouts  0.8 us (3%)
    pallas_call x1, Pallas kernels, body(): pl.pallas_call(functools.partial(kernel, sizes), out_shape=jax.ShapeDtype...  29.2 us
    unnamed x1, local copies, waits for them, and re-layouts  0.8 us

profile of v4, /device:TPU:1, one launch (start us, length us, event | category | flops | bytes accessed | tf_op | source)
XLA Modules:
  0.0 30.0 jit_solution(5562160016642129103)
XLA Ops:
  0.0 29.2 %shard_map.46 = f32[4,256,128]{2,1,0:T(8,128)S(1)} custom-call(f32[5,256,128]{2,1,0:T(8,128)} %bitcast.3, f32[8]{0:T(128)} %coriolis.1, f32[8,128]{1,0:T(8,128)} %slope_east.1, f32[8,128]{1,0:T(8,128)} %slope_north.1), custom_call_target="tpu_custom_call" | custom-call | tf_op jit(solution)/shard_map/pallas_call | solution.py:509
  29.2 0.8 %copy.6 = f32[4,32,8,128]{3,2,1,0:T(8,128)} copy(f32[4,32,8,128]{3,2,1,0:T(8,128)S(1)} %bitcast.2) | data formatting | bytes 1048576

commit v5 on v4

--- a/solution.py
+++ b/solution.py
@@ -71,8 +71,8 @@
 def kernel(
     sizes, fields, coriolis, slope_east, slope_north, out,
     zf, xt, ysend, yrecv, halo, csend, crecv, eddy_y, eddy_z, eddy_v, eddy_x, xdiv, east, north, cor,
-    recv_a, recv_z, recv_y,
-    load_sem, send_a, got_a, send_z, got_z, send_y, got_y, send_h, got_h, vouch,
+    recv_a, recv_q,
+    load_sem, send_a, got_a, send_q, got_q, send_h, got_h, vouch,
 ):
     nx, nl, nc, nh, nz = sizes
     ny = nh * nl
@@ -131,9 +131,14 @@
         h = lax.div(i, nl)
         return (px, i - h * nl, pc, h, pz)
 
+    def at_q(y, z):
+        return (*at_y(y)[:4], z)
+
     n_a = nx * nc
     pa, py = px * nc + pc, ph * nl + pl_
-    near_y = [carry(py + d, ny)[0] for d in range(1, ny) if min(d, ny - d) <= NEAR_Y]
+    pq = py * nz + pz
+    around = [(min(d, ny - d) <= NEAR_Y, carry(py + d, ny)[0]) for d in range(1, ny)]
+    near_y, far_y = [y for near, y in around if near], [y for near, y in around if not near]
     gx_low, gx_high = along_gx(step_down), along_gx(step_up)
     gy_low, gy_high = along_gy(step_down), along_gy(step_up)
 
@@ -193,10 +198,10 @@
 
     def total_of(rows, got):
         all_of(others(rows), got)
-        value = rows[0]
-        for i in range(1, rows.shape[0]):
-            value = value + rows[i]
-        return value
+        parts = [rows[i] for i in range(rows.shape[0])]
+        while len(parts) > 1:
+            parts = [sum(parts[i : i + 2][1:], parts[i]) for i in range(0, len(parts), 2)]
+        return parts[0]
 
     for copy in loads[1:]:
         copy.wait()
@@ -239,11 +244,8 @@
     remote(ysend.at[1], yrecv.at[0], send_h.at[0], got_h.at[0], gx_high).start()
     pl.when(pz == nz - 1)(functools.partial(tell, vouch.at[1], gy_high))
     pl.when(pz > 0)(functools.partial(tell, vouch.at[0], gy_low))
-    each(0, pz, lambda i: tell(vouch.at[2], at_z(i)))
-    far_y = ny > 2 * NEAR_Y
-    if far_y:
-        for d in (NEAR_Y, ny - NEAR_Y):
-            tell(vouch.at[3], at_y(carry(py + d, ny)[0]))
+    for y in near_y:
+        tell(vouch.at[2], at_y(y))
 
     turning = jnp.zeros((ROWS, LANES), jnp.float32)
     for j in range(ROWS):
@@ -280,19 +282,34 @@
 
     lax.fori_loop(0, groups, upright, 0)
 
-    recv_z[pz] = total_of(recv_a, got_a)
-    to_z = send_row(recv_z, pz, send_z, got_z, at_z)
-    each(0, pz, to_z)
+    if near_y:
+        pl.semaphore_wait(vouch.at[2], len(near_y))
+    each(0, pz, lambda i: tell(vouch.at[4], at_z(i)))
+    if far_y:
+        for d in (NEAR_Y, ny - NEAR_Y):
+            tell(vouch.at[3], at_y(carry(py + d, ny)[0]))
+
+    recv_q[pq] = total_of(recv_a, got_a)
+
+    def to_q(y, z):
+        remote(recv_q.at[pq], recv_q.at[pq], send_q, got_q, at_q(y, z)).start()
+
+    def to_columns(columns):
+        def visit(z):
+            for y in columns:
+                to_q(y, z)
+
+        return visit
+
+    if far_y:
+        pl.semaphore_wait(vouch.at[3], 2)
+    each(0, pz, to_columns([py, *near_y, *far_y]))
+    to_columns(near_y + far_y)(pz)
 
     @pl.when(pz < nz - 1)
     def _():
         pl.semaphore_wait(vouch.at[0], 1)
         x_copies[1].start()
-
-    @pl.when(pz < nz - 1)
-    def _():
-        pl.semaphore_wait(vouch.at[2], nz - 1 - pz)
-        each(pz + 1, nz, to_z)
 
     @pl.when(pz == 0)
     def _():
@@ -349,6 +366,11 @@
         return carry
 
     lax.fori_loop(0, 2 * halves, eastward, 0)
+
+    @pl.when(pz < nz - 1)
+    def _():
+        pl.semaphore_wait(vouch.at[4], nz - 1 - pz)
+        each(pz + 1, nz, to_columns([py, *near_y, *far_y]))
 
     all_of(yrecv, got_h.at[0])
     for side, at_edge in ((0, gx == 0), (1, gx == n_gx - 1)):
@@ -392,12 +414,43 @@
 
     lax.fori_loop(0, groups, northward, 0)
 
-    recv_y[py] = total_of(recv_z, got_z)
-    if far_y:
-        pl.semaphore_wait(vouch.at[3], 2)
-    to_y = send_row(recv_y, py, send_y, got_y, at_y)
-    for i in range(1, ny):
-        to_y(carry(py + i, ny)[0])
+    def across(inner, outer):
+        plus = pltpu.roll(jnp.where(lane == 0, outer, inner), LANES - 1, 1)
+        minus = pltpu.roll(jnp.where(lane == LANES - 1, outer, inner), 1, 1)
+        return plus - minus
+
+    def eddy_row(j, g):
+        u, v = row(0, j, g), row(1, j, g)
+        ux, vx = across(u, halo_row(0, j, g)), across(v, halo_row(1, j, g))
+        uy, vy = row(0, j + 1, g) - row(0, j - 1, g), row(1, j + 1, g) - row(1, j - 1, g)
+        e = strength(ux, vx, uy, vy)
+        eddy_y[j + 1, pl.ds(g * ROWS, ROWS), :] = e
+        if 0 <= j < ROWS:
+            eddy_z[pl.ds(g * 64 + j, ROWS, stride=ROWS), :] = e
+
+    def eddy_side(j, g):
+        ux, vx = across(halo_row(0, j, g), row(0, j, g)), across(halo_row(1, j, g), row(1, j, g))
+        uy = halo_row(0, j + 1, g) - halo_row(0, j - 1, g)
+        vy = halo_row(1, j + 1, g) - halo_row(1, j - 1, g)
+        eddy_v[pl.ds(g * 64 + j, ROWS, stride=ROWS), :] = strength(ux, vx, uy, vy)
+
+    def eddies_inside(g, carry):
+        for j in range(ROWS):
+            eddy_row(j, g)
+        for j in range(1, ROWS - 1):
+            eddy_side(j, g)
+        return carry
+
+    def eddies_rim(g, carry):
+        for j in (-1, ROWS):
+            eddy_row(j, g)
+        for j in (0, ROWS - 1):
+            eddy_side(j, g)
+        return carry
+
+    lax.fori_loop(0, groups, eddies_inside, 0)
+    for half in range(halves):
+        eddy_x[half, pl.ds(ROWS, LANES), :] = eddy_z[pl.ds(half * LANES, LANES), :].T
 
     all_of(crecv, got_h.at[1])
     for side, at_edge in ((0, gx == 0), (1, gx == n_gx - 1)):
@@ -406,33 +459,8 @@
         def _():
             crecv[side] = jnp.zeros(crecv.shape[1:], jnp.float32)
 
-    def eddies(g, carry):
-        u = [row(0, j, g) for j in range(-2, ROWS + 2)]
-        v = [row(1, j, g) for j in range(-2, ROWS + 2)]
-        hu = [halo_row(0, j, g) for j in range(-1, ROWS + 1)]
-        hv = [halo_row(1, j, g) for j in range(-1, ROWS + 1)]
-        left, right = lane == LANES - 1, lane == 0
-
-        def across(inner, outer):
-            plus = pltpu.roll(jnp.where(right, outer, inner), LANES - 1, 1)
-            minus = pltpu.roll(jnp.where(left, outer, inner), 1, 1)
-            return plus - minus
-
-        for j in range(-1, ROWS + 1):
-            ux, vx = across(u[j + 2], hu[j + 1]), across(v[j + 2], hv[j + 1])
-            uy, vy = u[j + 3] - u[j + 1], v[j + 3] - v[j + 1]
-            e = strength(ux, vx, uy, vy)
-            eddy_y[j + 1, pl.ds(g * ROWS, ROWS), :] = e
-            if 0 <= j < ROWS:
-                eddy_z[pl.ds(g * 64 + j, ROWS, stride=ROWS), :] = e
-                ux, vx = across(hu[j + 1], u[j + 2]), across(hv[j + 1], v[j + 2])
-                uy, vy = hu[j + 2] - hu[j], hv[j + 2] - hv[j]
-                eddy_v[pl.ds(g * 64 + j, ROWS, stride=ROWS), :] = strength(ux, vx, uy, vy)
-        return carry
-
-    lax.fori_loop(0, groups, eddies, 0)
+    lax.fori_loop(0, groups, eddies_rim, 0)
     for half in range(halves):
-        eddy_x[half, pl.ds(ROWS, LANES), :] = eddy_z[pl.ds(half * LANES, LANES), :].T
         outer = eddy_v[pl.ds(half * LANES, LANES), :].T
         eddy_x[half, pl.ds(0, ROWS), :] = outer[LANES - ROWS :]
         eddy_x[half, pl.ds(ROWS + LANES, ROWS), :] = outer[:ROWS]
@@ -477,7 +505,7 @@
             rows = pl.ds(half * LANES, LANES)
             out[f, rows, :] = out[f, rows, :] + xdiv[f, half].T
 
-    own = total_of(recv_y, got_y)
+    own = total_of(recv_q, got_q)
     scale = SECTION_DT * BUOYANCY / (n_gx * ROWS * n_gy * LANES)
     for g in range(groups):
         mean = jnp.sum(jnp.where(lane == sub + ROWS * g, own * scale, 0.0), axis=1, keepdims=True)
@@ -487,8 +515,7 @@
 
     for ref, sem in (
         (others(recv_a), send_a),
-        (others(recv_z), send_z),
-        (others(recv_y), send_y),
+        (others(recv_q), send_q),
         (ysend, send_h.at[0]),
         (csend, send_h.at[1]),
     ):
@@ -528,10 +555,8 @@
             pltpu.VMEM((ROWS, LANES), f32),
             pltpu.SMEM((ROWS,), f32),
             pltpu.VMEM((nx * nc, 1, LANES), f32),
-            pltpu.VMEM((nz, 1, LANES), f32),
-            pltpu.VMEM((nl * nh, 1, LANES), f32),
-            dma((6,)), dma, dma, dma, dma, dma, dma, dma((4,)), dma((4,)),
-            pltpu.SemaphoreType.REGULAR((4,)),
+            pltpu.VMEM((nl * nh * nz, 1, LANES), f32),
+            dma((6,)), dma, dma, dma, dma, dma((4,)), dma((4,)), pltpu.SemaphoreType.REGULAR((5,)),
         ],
         compiler_params=pltpu.CompilerParams(
             collective_id=0, has_side_effects=True, vmem_limit_bytes=24 * 1024 * 1024

time: 30.2 us -> 29.8 us (0.987)
  Pallas kernels: 29.2 us -> 28.8 us
    pallas_call x1, Pallas kernels: 29.2 us -> 28.8 us  [body(): pl.pallas_call(functools.partial(kernel, sizes), out_shape=jax.ShapeDtype...]
where the time goes in v5:
time: 29.8 us; the launch traced here: 29.6 us
  Pallas kernels  28.8 us (97%)
  local copies, waits for them, and re-layouts  0.8 us (3%)
    pallas_call x1, Pallas kernels, body(): pl.pallas_call(functools.partial(kernel, sizes), out_shape=jax.ShapeDtype...  28.8 us
    unnamed x1, local copies, waits for them, and re-layouts  0.8 us

profile of v5, /device:TPU:1, one launch (start us, length us, event | category | flops | bytes accessed | tf_op | source)
XLA Modules:
  0.0 29.6 jit_solution(5432918535134721250)
XLA Ops:
  0.0 28.8 %shard_map.46 = f32[4,256,128]{2,1,0:T(8,128)S(1)} custom-call(f32[5,256,128]{2,1,0:T(8,128)} %bitcast.3, f32[8]{0:T(128)} %coriolis.1, f32[8,128]{1,0:T(8,128)} %slope_east.1, f32[8,128]{1,0:T(8,128)} %slope_north.1), custom_call_target="tpu_custom_call" | custom-call | tf_op jit(solution)/shard_map/pallas_call | solution.py:536
  28.8 0.8 %copy.6 = f32[4,32,8,128]{3,2,1,0:T(8,128)} copy(f32[4,32,8,128]{3,2,1,0:T(8,128)S(1)} %bitcast.2) | data formatting | bytes 1048576

commit v6 on v5

--- a/solution.py
+++ b/solution.py
@@ -22,6 +22,7 @@
 LANES = 128
 ROWS = 8
 NEAR_Y = 2
+CORNER = 16
 EDGE = 24
 
 
@@ -70,7 +71,7 @@
 
 def kernel(
     sizes, fields, coriolis, slope_east, slope_north, out,
-    zf, xt, ysend, yrecv, halo, csend, crecv, eddy_y, eddy_z, eddy_v, eddy_x, xdiv, east, north, cor,
+    zf, xt, ysend, yrecv, halo, csend, crecv, corner, eddy_y, eddy_z, eddy_v, eddy_x, xdiv, east, north, cor,
     recv_a, recv_q,
     load_sem, send_a, got_a, send_q, got_q, send_h, got_h, vouch,
 ):
@@ -157,14 +158,13 @@
     def tell(sem, peer):
         pl.semaphore_signal(sem, inc=1, device_id=peer, device_id_type=MESH)
 
-    together = [at_y(y) for y in near_y] + [gx_low, gx_high]
+    by_distance = sorted(range(1, n_a), key=lambda i: -min(i // nc, nx - i // nc))
+    together = [at_a(carry(pa + i, n_a)[0]) for i in by_distance] + [at_y(y) for y in near_y] + [gx_low, gx_high]
     for peer in together:
         tell(barrier, peer)
-    for i in range(1, n_a):
-        tell(barrier, at_a(carry(pa + i, n_a)[0]))
     each(pz + 1, nz, lambda i: tell(barrier, at_z(i)))
     pl.when(pz == 0)(functools.partial(tell, barrier, gy_low))
-    expected = len(together) + n_a - 1 + pz + one(pz == nz - 1)
+    expected = len(together) + pz + one(pz == nz - 1)
 
     lane = lax.broadcasted_iota(jnp.int32, (ROWS, LANES), 1)
     sub = lax.broadcasted_iota(jnp.int32, (ROWS, LANES), 0)
@@ -230,8 +230,10 @@
 
     pl.semaphore_wait(barrier, expected)
     to_a = send_row(recv_a, pa, send_a, got_a, at_a)
-    for i in range(1, n_a):
+    for i in by_distance:
         to_a(carry(pa + i, n_a)[0])
+    for y in near_y:
+        tell(vouch.at[2], at_y(y))
     tile_low, tile_high = xt.at[:, :, pl.ds(ROWS, ROWS)], xt.at[:, :, pl.ds(LANES, ROWS)]
     past_low, past_high = xt.at[:, :, pl.ds(0, ROWS)], xt.at[:, :, pl.ds(ROWS + LANES, ROWS)]
     x_copies = [
@@ -240,13 +242,14 @@
     ]
     pl.when(pz == nz - 1)(x_copies[1].start)
     pl.when(pz > 0)(x_copies[0].start)
-    remote(ysend.at[0], yrecv.at[1], send_h.at[0], got_h.at[0], gx_low).start()
-    remote(ysend.at[1], yrecv.at[0], send_h.at[0], got_h.at[0], gx_high).start()
+
+    def send_rows():
+        remote(ysend.at[0], yrecv.at[1], send_h.at[0], got_h.at[0], gx_low).start()
+        remote(ysend.at[1], yrecv.at[0], send_h.at[0], got_h.at[0], gx_high).start()
+
+    pl.when(pz < nz // 2)(send_rows)
     pl.when(pz == nz - 1)(functools.partial(tell, vouch.at[1], gy_high))
     pl.when(pz > 0)(functools.partial(tell, vouch.at[0], gy_low))
-    for y in near_y:
-        tell(vouch.at[2], at_y(y))
-
     turning = jnp.zeros((ROWS, LANES), jnp.float32)
     for j in range(ROWS):
         turning = jnp.where(sub == j, cor[j] * SECTION_DT, turning)
@@ -284,7 +287,11 @@
 
     if near_y:
         pl.semaphore_wait(vouch.at[2], len(near_y))
-    each(0, pz, lambda i: tell(vouch.at[4], at_z(i)))
+    close = nz // 2 - 1
+    split = jnp.maximum(pz - close, 0)
+    each(split, pz, lambda i: tell(vouch.at[4], at_z(i)))
+    each(0, split, lambda i: tell(vouch.at[5], at_z(i)))
+    last_close = jnp.minimum(pz + close, nz - 1)
     if far_y:
         for d in (NEAR_Y, ny - NEAR_Y):
             tell(vouch.at[3], at_y(carry(py + d, ny)[0]))
@@ -301,76 +308,21 @@
 
         return visit
 
+    ahead = jnp.minimum(pz, 2) if far_y else pz
+    each(0, ahead, to_columns([py, *near_y]))
     if far_y:
         pl.semaphore_wait(vouch.at[3], 2)
-    each(0, pz, to_columns([py, *near_y, *far_y]))
+        each(0, ahead, to_columns(far_y))
+        each(ahead, pz, to_columns([py, *near_y, *far_y]))
     to_columns(near_y + far_y)(pz)
+    pl.when(pz >= nz // 2)(send_rows)
 
     @pl.when(pz < nz - 1)
     def _():
         pl.semaphore_wait(vouch.at[0], 1)
         x_copies[1].start()
-
-    @pl.when(pz == 0)
-    def _():
-        pl.semaphore_wait(vouch.at[1], 1)
-        x_copies[0].start()
-
-    for copy in x_copies:
-        copy.wait_recv()
-
-    edge_rows = jnp.zeros((5, halves, ROWS, LANES), jnp.float32)
-
-    @pl.when(gy == 0)
-    def _():
-        xt[:, :, pl.ds(0, ROWS), :] = edge_rows
-
-    @pl.when(gy == n_gy - 1)
-    def _():
-        xt[:, :, pl.ds(ROWS + LANES, ROWS), :] = edge_rows
-
-    gap = jnp.zeros((LANES - 2 * ROWS, LANES), jnp.float32)
-    for f in range(2):
-        for half in range(halves):
-            block = jnp.concatenate(
-                [xt[f, half, pl.ds(ROWS + LANES, ROWS), :], gap, xt[f, half, pl.ds(0, ROWS), :]], axis=0
-            )
-            halo[f, pl.ds(half * LANES, LANES), :] = block.T
-    for f in range(2):
-        csend[0, f] = halo[f, pl.ds(0, depth, stride=ROWS), :]
-        csend[1, f] = halo[f, pl.ds(7, depth, stride=ROWS), :]
-
-    remote(csend.at[0], crecv.at[1], send_h.at[1], got_h.at[1], gx_low).start()
-    remote(csend.at[1], crecv.at[0], send_h.at[1], got_h.at[1], gx_high).start()
-    step = LANES // ROWS
-
-    def eastward(c, carry):
-        half, start = c // 2, lax.rem(c, 2) * ROWS
-
-        def cells(f, first=-3, count=ROWS + 6):
-            return [
-                xt[f, half, pl.ds(start + (ROWS + first + i), ROWS, stride=step), :] for i in range(count)
-            ]
-
-        u = cells(0)
-        sigma, size, upward = speeds(u)
-        p = cells(4, -1, ROWS + 2)
-        for f in range(4):
-            q = u if f == 0 else cells(f)
-            flux = line_terms(q, sigma, size, upward)
-            for i in range(ROWS):
-                value = flux[i + 1] - flux[i]
-                if f == 0:
-                    value = value - (p[i + 2] - p[i]) * (0.5 * SECTION_DT)
-                xdiv[f, half, pl.ds(start + i, ROWS, stride=step), :] = value
-        return carry
-
-    lax.fori_loop(0, 2 * halves, eastward, 0)
-
-    @pl.when(pz < nz - 1)
-    def _():
-        pl.semaphore_wait(vouch.at[4], nz - 1 - pz)
-        each(pz + 1, nz, to_columns([py, *near_y, *far_y]))
+        pl.semaphore_wait(vouch.at[4], last_close - pz)
+        each(pz + 1, last_close + 1, to_columns([py, *near_y, *far_y]))
 
     all_of(yrecv, got_h.at[0])
     for side, at_edge in ((0, gx == 0), (1, gx == n_gx - 1)):
@@ -387,11 +339,9 @@
         return strided(zf, f, EDGE + g * 64 + j)
 
     def halo_row(f, j, g):
-        if j < 0:
-            return crecv[0, f, pl.ds(g * ROWS, ROWS), :]
-        if j >= ROWS:
-            return crecv[1, f, pl.ds(g * ROWS, ROWS), :]
-        return strided(halo, f, g * 64 + j)
+        if 0 <= j < ROWS:
+            return strided(halo, f, g * 64 + j)
+        return corner[0 if j < 0 else 1, f, pl.ds(g * ROWS, ROWS), :]
 
     def strength(ux, vx, uy, vy):
         cross = uy + vx
@@ -414,6 +364,66 @@
 
     lax.fori_loop(0, groups, northward, 0)
 
+    @pl.when(pz == 0)
+    def _():
+        pl.semaphore_wait(vouch.at[1], 1)
+        x_copies[0].start()
+
+    for copy in x_copies:
+        copy.wait_recv()
+
+    edge_rows = jnp.zeros((5, halves, ROWS, LANES), jnp.float32)
+
+    @pl.when(gy == 0)
+    def _():
+        xt[:, :, pl.ds(0, ROWS), :] = edge_rows
+
+    @pl.when(gy == n_gy - 1)
+    def _():
+        xt[:, :, pl.ds(ROWS + LANES, ROWS), :] = edge_rows
+
+    gap = jnp.zeros((LANES - 2 * ROWS, LANES), jnp.float32)
+    for f in range(2):
+        for half in range(halves):
+            block = jnp.concatenate(
+                [xt[f, half, pl.ds(ROWS + LANES, ROWS), :], gap, xt[f, half, pl.ds(0, ROWS), :]], axis=0
+            )
+            halo[f, pl.ds(half * LANES, LANES), :] = block.T
+    place = lax.rem(lane + CORNER // 2, LANES) // CORNER
+    for side, j in ((0, 0), (1, ROWS - 1)):
+        packed = jnp.zeros((ROWS, LANES), jnp.float32)
+        for m in range(2 * groups):
+            piece = strided(halo, m // groups, (m % groups) * 64 + j)
+            packed = jnp.where(place == m, pltpu.roll(piece, m * CORNER, 1) if m else piece, packed)
+        csend[side] = packed
+
+    remote(csend.at[0], crecv.at[1], send_h.at[1], got_h.at[1], gx_low).start()
+    remote(csend.at[1], crecv.at[0], send_h.at[1], got_h.at[1], gx_high).start()
+    step = LANES // ROWS
+
+    def eastward(c, carry):
+        half, start = c // 2, lax.rem(c, 2) * ROWS
+
+        def cells(f, first=-3, count=ROWS + 6):
+            return [
+                xt[f, half, pl.ds(start + (ROWS + first + i), ROWS, stride=step), :] for i in range(count)
+            ]
+
+        u = cells(0)
+        sigma, size, upward = speeds(u)
+        p = cells(4, -1, ROWS + 2)
+        for f in range(4):
+            q = u if f == 0 else cells(f)
+            flux = line_terms(q, sigma, size, upward)
+            for i in range(ROWS):
+                value = flux[i + 1] - flux[i]
+                if f == 0:
+                    value = value - (p[i + 2] - p[i]) * (0.5 * SECTION_DT)
+                xdiv[f, half, pl.ds(start + i, ROWS, stride=step), :] = value
+        return carry
+
+    lax.fori_loop(0, 2 * halves, eastward, 0)
+
     def across(inner, outer):
         plus = pltpu.roll(jnp.where(lane == 0, outer, inner), LANES - 1, 1)
         minus = pltpu.roll(jnp.where(lane == LANES - 1, outer, inner), 1, 1)
@@ -452,12 +462,23 @@
     for half in range(halves):
         eddy_x[half, pl.ds(ROWS, LANES), :] = eddy_z[pl.ds(half * LANES, LANES), :].T
 
+    @pl.when(last_close < nz - 1)
+    def _():
+        pl.semaphore_wait(vouch.at[5], nz - 1 - last_close)
+        each(last_close + 1, nz, to_columns([py, *near_y, *far_y]))
+
     all_of(crecv, got_h.at[1])
     for side, at_edge in ((0, gx == 0), (1, gx == n_gx - 1)):
 
         @pl.when(at_edge)
         def _():
             crecv[side] = jnp.zeros(crecv.shape[1:], jnp.float32)
+
+    for side in range(2):
+        packed = crecv[side]
+        for m in range(2 * groups):
+            piece = pltpu.roll(packed, LANES - m * CORNER, 1) if m else packed
+            corner[side, m // groups, pl.ds((m % groups) * ROWS, ROWS), :] = piece
 
     lax.fori_loop(0, groups, eddies_rim, 0)
     for half in range(halves):
@@ -544,7 +565,8 @@
             pltpu.VMEM((2, 13, depth, LANES), f32),
             pltpu.VMEM((2, 13, depth, LANES), f32),
             pltpu.VMEM((2, cells, LANES), f32),
-            pltpu.VMEM((2, 2, depth, LANES), f32),
+            pltpu.VMEM((2, ROWS, LANES), f32),
+            pltpu.VMEM((2, ROWS, LANES), f32),
             pltpu.VMEM((2, 2, depth, LANES), f32),
             pltpu.VMEM((ROWS + 2, depth, LANES), f32),
             pltpu.VMEM((cells, LANES), f32),
@@ -556,7 +578,7 @@
             pltpu.SMEM((ROWS,), f32),
             pltpu.VMEM((nx * nc, 1, LANES), f32),
             pltpu.VMEM((nl * nh * nz, 1, LANES), f32),
-            dma((6,)), dma, dma, dma, dma, dma((4,)), dma((4,)), pltpu.SemaphoreType.REGULAR((5,)),
+            dma((6,)), dma, dma, dma, dma, dma((4,)), dma((4,)), pltpu.SemaphoreType.REGULAR((6,)),
         ],
         compiler_params=pltpu.CompilerParams(
             collective_id=0, has_side_effects=True, vmem_limit_bytes=24 * 1024 * 1024

time: 29.8 us -> 29.6 us (level)
  no operation moved by 1% of the time
where the time goes in v6:
time: 29.6 us; the launch traced here: 29.4 us
  Pallas kernels  28.6 us (97%)
  local copies, waits for them, and re-layouts  0.8 us (3%)
    pallas_call x1, Pallas kernels, body(): pl.pallas_call(functools.partial(kernel, sizes), out_shape=jax.ShapeDtype...  28.6 us
    unnamed x1, local copies, waits for them, and re-layouts  0.8 us

profile of v6, /device:TPU:1, one launch (start us, length us, event | category | flops | bytes accessed | tf_op | source)
XLA Modules:
  0.0 29.4 jit_solution(17274188932807061037)
XLA Ops:
  0.0 28.6 %shard_map.46 = f32[4,256,128]{2,1,0:T(8,128)S(1)} custom-call(f32[5,256,128]{2,1,0:T(8,128)} %bitcast.3, f32[8]{0:T(128)} %coriolis.1, f32[8,128]{1,0:T(8,128)} %slope_east.1, f32[8,128]{1,0:T(8,128)} %slope_north.1), custom_call_target="tpu_custom_call" | custom-call | tf_op jit(solution)/shard_map/pallas_call | solution.py:557
  28.6 0.8 %copy.6 = f32[4,32,8,128]{3,2,1,0:T(8,128)} copy(f32[4,32,8,128]{3,2,1,0:T(8,128)S(1)} %bitcast.2) | data formatting | bytes 1048576

commit v7 on v6

--- a/solution.py
+++ b/solution.py
@@ -87,10 +87,10 @@
     loads = [
         pltpu.make_async_copy(fields.at[3], zf.at[3, main], load_sem.at[0]),
         pltpu.make_async_copy(fields.at[winds], zf.at[winds, main], load_sem.at[1]),
-        pltpu.make_async_copy(fields.at[4], zf.at[4, main], load_sem.at[2]),
-        pltpu.make_async_copy(slope_east, east, load_sem.at[3]),
-        pltpu.make_async_copy(slope_north, north, load_sem.at[4]),
-        pltpu.make_async_copy(coriolis, cor, load_sem.at[5]),
+        pltpu.make_async_copy(fields.at[4], zf.at[4, main], load_sem.at[1]),
+        pltpu.make_async_copy(slope_east, east, load_sem.at[2]),
+        pltpu.make_async_copy(slope_north, north, load_sem.at[3]),
+        pltpu.make_async_copy(coriolis, cor, load_sem.at[4]),
     ]
     for copy in loads:
         copy.start()
@@ -159,7 +159,10 @@
         pl.semaphore_signal(sem, inc=1, device_id=peer, device_id_type=MESH)
 
     by_distance = sorted(range(1, n_a), key=lambda i: -min(i // nc, nx - i // nc))
-    together = [at_a(carry(pa + i, n_a)[0]) for i in by_distance] + [at_y(y) for y in near_y] + [gx_low, gx_high]
+    far_first = sorted(range(1, ny), key=lambda d: (-min(d, ny - d), -d))
+    steps = [d for d in far_first if min(d, ny - d) <= NEAR_Y]
+    together = [at_y(carry(py + d, ny)[0]) for d in steps]
+    together += [at_a(carry(pa + i, n_a)[0]) for i in by_distance] + [gx_low, gx_high]
     for peer in together:
         tell(barrier, peer)
     each(pz + 1, nz, lambda i: tell(barrier, at_z(i)))
@@ -203,7 +206,8 @@
             parts = [sum(parts[i : i + 2][1:], parts[i]) for i in range(0, len(parts), 2)]
         return parts[0]
 
-    for copy in loads[1:]:
+    all_of(zf.at[pl.ds(0, 4), main], load_sem.at[1])
+    for copy in loads[3:]:
         copy.wait()
 
     for f in range(5):
@@ -578,7 +582,7 @@
             pltpu.SMEM((ROWS,), f32),
             pltpu.VMEM((nx * nc, 1, LANES), f32),
             pltpu.VMEM((nl * nh * nz, 1, LANES), f32),
-            dma((6,)), dma, dma, dma, dma, dma((4,)), dma((4,)), pltpu.SemaphoreType.REGULAR((6,)),
+            dma((5,)), dma, dma, dma, dma, dma((4,)), dma((4,)), pltpu.SemaphoreType.REGULAR((6,)),
         ],
         compiler_params=pltpu.CompilerParams(
             collective_id=0, has_side_effects=True, vmem_limit_bytes=24 * 1024 * 1024

time: 29.6 us -> 29.6 us (level)
  no operation moved by 1% of the time
where the time goes in v7:
time: 29.6 us; the launch traced here: 29.5 us
  Pallas kernels  28.7 us (97%)
  local copies, waits for them, and re-layouts  0.8 us (3%)
    pallas_call x1, Pallas kernels, body(): pl.pallas_call(functools.partial(kernel, sizes), out_shape=jax.ShapeDtype...  28.7 us
    unnamed x1, local copies, waits for them, and re-layouts  0.8 us

profile of v7, /device:TPU:1, one launch (start us, length us, event | category | flops | bytes accessed | tf_op | source)
XLA Modules:
  0.0 29.5 jit_solution(16211214228018475730)
XLA Ops:
  0.0 28.7 %shard_map.46 = f32[4,256,128]{2,1,0:T(8,128)S(1)} custom-call(f32[5,256,128]{2,1,0:T(8,128)} %bitcast.3, f32[8]{0:T(128)} %coriolis.1, f32[8,128]{1,0:T(8,128)} %slope_east.1, f32[8,128]{1,0:T(8,128)} %slope_north.1), custom_call_target="tpu_custom_call" | custom-call | tf_op jit(solution)/shard_map/pallas_call | solution.py:561
  28.7 0.8 %copy.6 = f32[4,32,8,128]{3,2,1,0:T(8,128)} copy(f32[4,32,8,128]{3,2,1,0:T(8,128)S(1)} %bitcast.2) | data formatting | bytes 1048576
